TPU v7x, 256 devices: a whole 4x4x8 slice. The times are simulated.
256 devices in a mesh: seq: 128 (over z_lo, y, x, core), head: 2 (over z_hi).
Axes of the slice: x: 4, y: 4, z: 8 (z_hi: 2, z_lo: 4; z = z_hi * 4 + z_lo), core: 2. Of those that a mesh axis runs over, the one named last changes fastest.
Arguments:
- queries: bfloat16 [16384, 2048], P('seq', 'head'), may hold values from -144 to 144
- keys: bfloat16 [16384, 2048], P('seq', 'head'), may hold values from -4 to 4
- values: bfloat16 [16384, 2048], P('seq', 'head'), may hold values from -6 to 6
- grad_out: bfloat16 [16384, 2048], P('seq', 'head'), may hold values from -6 to 6
- bias_table: float32 [32, 128], P('head'), may hold values from -5 to 5
- bucket_ids: int32 [128, 4, 256], P('seq'), may hold values from 0 to 127
- block_mask: int32 [128, 4], P('seq'), may hold values 0 or 1
Outputs:
- grad_queries: bfloat16 [16384, 2048], P('seq', 'head')
- grad_keys: bfloat16 [16384, 2048], P('seq', 'head')
- grad_values: bfloat16 [16384, 2048], P('seq', 'head')
- grad_bias: float32 [32, 128], replicated
All inputs are finite; a program needn't handle non-finite values. No bound on the sum of `block_mask` on one device may be relied on, other than what follows from the above.
Results may differ from a plain program's by a relative error of at most 0.005.
Values may be sent and summed in bfloat16 or wider, within the bound.
A program may use at most 64 MiB of HBM per device.

v0:
```python
import functools

import jax
import jax.numpy as jnp
from jax import lax
from jax.sharding import Mesh
from jax.sharding import PartitionSpec as P

SEQ = ("seq_0", "seq_1", "seq_2", "seq_3")


def passed_along(value, axis, by):
    devices = lax.axis_size(axis)
    pairs = [(i, i + by) for i in range(devices) if 0 <= i + by < devices]
    return lax.ppermute(value, axis, pairs)


def over_axes(value, axes):
    return functools.reduce(lax.psum, axes, value)


def laid_out(blocks, dim):
    shape = list(blocks.shape[1:])
    shape[dim] *= blocks.shape[0]
    return jnp.moveaxis(blocks, 0, dim).reshape(shape)


def sent_to_all(value, axis):
    copies = jnp.broadcast_to(value, (lax.axis_size(axis), *value.shape))
    return lax.all_to_all(copies, axis, split_axis=0, concat_axis=0, tiled=True)


def gathered_copies(value, axis, dim):
    return laid_out(sent_to_all(value, axis), dim)


def diagonal_sums(field):
    heads, rows, _ = field.shape
    flipped = field[:, :, ::-1]
    padded = jnp.pad(flipped, ((0, 0), (0, 0), (0, rows)))
    sheared = padded.reshape(heads, 2 * rows * rows)[:, : rows * (2 * rows - 1)]
    sums = sheared.reshape(heads, rows, 2 * rows - 1).sum(axis=1)
    return jnp.pad(sums, ((0, 0), (0, 1)))


def toeplitz_rows(by_offset, rows):
    heads = by_offset.shape[0]
    reverse = by_offset[:, : 2 * rows - 1][:, ::-1]
    tiled = jnp.tile(reverse, (1, rows))
    window = tiled[:, rows - 1 : rows - 1 + rows * (2 * rows - 2)]
    return window.reshape(heads, rows, 2 * rows - 2)[:, :, :rows]


def body(queries, keys, values, grad_out, bias_table, bucket_ids, block_mask):
    tok, width = queries.shape
    heads, buckets = bias_table.shape
    head_dim = width // heads
    span = block_mask.shape[1]
    scale = head_dim ** (-0.5)
    highest = lax.Precision.HIGHEST
    index = lax.axis_index(SEQ)
    query_heads = queries.reshape(tok, heads, head_dim)
    cot_heads = grad_out.reshape(tok, heads, head_dim)
    rows = jnp.arange(tok, dtype=jnp.int32)
    lower = rows[:, None] >= rows[None, :]
    codes = jnp.arange(buckets, dtype=jnp.int32)
    table_ids = bucket_ids[0]
    flags = block_mask[0]

    def pair_terms(key_blk, value_blk, step):
        ids = lax.dynamic_index_in_dim(table_ids, step, 0, keepdims=False)
        onehot = (ids[:, None] == codes[None, :]).astype(jnp.float32)
        by_offset = jnp.dot(bias_table, onehot.T, precision=highest)
        bias_full = toeplitz_rows(by_offset, tok)
        key_heads = key_blk.reshape(tok, heads, head_dim)
        value_heads = value_blk.reshape(tok, heads, head_dim)
        scores = (
            scale
            * jnp.einsum("qhd,khd->hqk", query_heads, key_heads, preferred_element_type=jnp.float32)
            + bias_full
        )
        dprob = jnp.einsum(
            "qhd,khd->hqk", cot_heads, value_heads, preferred_element_type=jnp.float32
        )
        flag = lax.dynamic_index_in_dim(flags, step, 0, keepdims=False)
        whole = (flag == 1) & (index - step >= 0)
        valid = jnp.where(step == 0, lower, whole)
        masked = jnp.where(valid[None], scores, jnp.float32(-1e30))
        return (onehot, key_heads, masked, valid, dprob)

    def forward_step(stats, key_blk, value_blk, step):
        most, total, accum = stats
        _, _, masked, valid, dprob = pair_terms(key_blk, value_blk, step)
        top = jnp.maximum(most, masked.max(axis=-1))
        weights = jnp.where(valid[None], jnp.exp(masked - top[..., None]), jnp.float32(0.0))
        factor = jnp.exp(most - top)
        return (
            top,
            total * factor + weights.sum(axis=-1),
            accum * factor + (weights * dprob).sum(axis=-1),
        )

    zeros_rows = jnp.zeros((heads, tok), jnp.float32)
    stats = forward_step(
        (jnp.full((heads, tok), -1e30, jnp.float32), zeros_rows, zeros_rows), keys, values, 0
    )
    stash = (
        jnp.zeros((span, tok, width), keys.dtype).at[0].set(keys),
        jnp.zeros((span, tok, width), values.dtype).at[0].set(values),
    )

    def forward_loop(step, carry):
        key_blk, value_blk, stats, stash = carry
        key_blk, value_blk = passed_along((key_blk, value_blk), SEQ, 1)
        stats = forward_step(stats, key_blk, value_blk, step)
        stash = (
            lax.dynamic_update_index_in_dim(stash[0], key_blk, step, 0),
            lax.dynamic_update_index_in_dim(stash[1], value_blk, step, 0),
        )
        return (key_blk, value_blk, stats, stash)

    _, _, stats, stash = lax.fori_loop(1, span, forward_loop, (keys, values, stats, stash))
    most, total, accum = stats
    lse = most + jnp.log(total)
    delta = accum / total

    def backward_terms(key_blk, value_blk, step):
        onehot, key_heads, masked, valid, dprob = pair_terms(key_blk, value_blk, step)
        prob = jnp.exp(masked - lse[..., None])
        dscore = prob * (dprob - delta[..., None])
        score16 = dscore.astype(jnp.bfloat16)
        prob16 = prob.astype(jnp.bfloat16)
        grad_q = scale * jnp.einsum(
            "hqk,khd->qhd", score16, key_heads, preferred_element_type=jnp.float32
        ).reshape(tok, width)
        grad_k = scale * jnp.einsum(
            "hqk,qhd->khd", score16, query_heads, preferred_element_type=jnp.float32
        ).reshape(tok, width)
        grad_v = jnp.einsum(
            "hqk,qhd->khd", prob16, cot_heads, preferred_element_type=jnp.float32
        ).reshape(tok, width)
        grad_b = jnp.dot(diagonal_sums(dscore), onehot, precision=highest)
        return (grad_q, grad_k, grad_v, grad_b)

    last = span - 1
    first_terms = backward_terms(stash[0][last], stash[1][last], last)

    def chain_loop(turn, carry):
        grad_q, grad_k, grad_v, grad_b = carry
        step = span - 2 - turn
        grad_k, grad_v = passed_along((grad_k, grad_v), SEQ, -1)
        key_blk = lax.dynamic_index_in_dim(stash[0], step, 0, keepdims=False)
        value_blk = lax.dynamic_index_in_dim(stash[1], step, 0, keepdims=False)
        more = backward_terms(key_blk, value_blk, step)
        return (grad_q + more[0], grad_k + more[1], grad_v + more[2], grad_b + more[3])

    grad_q, grad_k, grad_v, grad_b = lax.fori_loop(0, span - 1, chain_loop, first_terms)
    key_grad = grad_k.astype(jnp.bfloat16)
    value_grad = grad_v.astype(jnp.bfloat16)
    summed = over_axes(grad_b, SEQ)
    grad_bias = gathered_copies(summed, "head", 0)
    return (grad_q.astype(jnp.bfloat16), key_grad, value_grad, grad_bias)


def solution(mesh):
    torus = Mesh(
        mesh.devices.reshape(4, 4, 4, 2, mesh.shape["head"]),
        ("seq_0", "seq_1", "seq_2", "seq_3", "head"),
    )
    placed = (
        P(SEQ, "head"),
        P(SEQ, "head"),
        P(SEQ, "head"),
        P(SEQ, "head"),
        P("head", None),
        P(SEQ, None, None),
        P(SEQ, None),
    )
    return jax.shard_map(
        body,
        mesh=torus,
        in_specs=placed,
        out_specs=(P(SEQ, "head"), P(SEQ, "head"), P(SEQ, "head"), P()),
        check_vma=False,
    )
```

profile of v0, /device:TPU:1, one launch (start us, length us, event | category | flops | bytes accessed | tf_op | source)
XLA Modules:
  0.0 286.6 jit_solution(12478347523809456802)
XLA Ops:
  5.7 2.5 tile.67
  8.2 2.2 slice.162
  10.4 4.6 %reshape.293 = f32[16,128,254]{2,1,0:T(8,128)} reshape(f32[16,32512]{1,0:T(8,128)S(1)} %slice.162) | data formatting | bytes 4161536 | tf_op jit(solution)/shard_map/reshape | solution.py:51
  19.4 2.1 scatter.9
  23.8 68.3 %while.52 = (s32[]{:T(128)}, bf16[128,1024]{0,1:T(8,128)(2,1)S(1)}, bf16[128,1024]{0,1:T(8,128)(2,1)}, f32[16,128]{1,0:T(8,128)S(1)}, f32[16,128]{1,0:T(8,128)S(...) while((s32[]{:T(128)}, bf16[128,1024]{0,1:T(8,128)(2,1)S(1)}, ...), condition=%wide.region_7.8_spmd.clone, body=%wide.region_3.7_spmd.clone.sunk | while | flops 76355592 | bytes 29592764 | solution.py:122
  23.8 4.5 %collective-permute-start = (bf16[128,1024]{0,1:T(8,128)(2,1)S(1)}, bf16[128,1024]{0,1:T(8,128)(2,1)S(1)}, u32[]{:S(2)}, u32[]{:S(2)}) collective-permute-start(bf16[128,1024]{0,1:T(8,128)(2,1)S(1)} %get-tuple-element.1186), channel_id=1, source_target_pairs={{0,2},{2,4},{4,6},{6,8},{8,10},{10,12},{12,14},{14,16},{16,18},{18... | collective-permute-start | bytes 786440 | tf_op jit(solution)/shard_map/while/body/eval_jaxpr/ppermute | solution.py:15
  28.3 1.9 collective-permute-start.1
  30.9 2.5 tile.79
  33.4 2.2 slice.180
  35.6 4.6 %reshape.315 = f32[16,128,254]{2,1,0:T(8,128)} reshape(f32[16,32512]{1,0:T(8,128)S(1)} %slice.180) | data formatting | bytes 4161536 | tf_op jit(solution)/shard_map/while/body/eval_jaxpr/reshape | solution.py:51
  47.3 3.5 %collective-permute-start = (bf16[128,1024]{0,1:T(8,128)(2,1)S(1)}, bf16[128,1024]{0,1:T(8,128)(2,1)S(1)}, u32[]{:S(2)}, u32[]{:S(2)}) collective-permute-start(bf16[128,1024]{0,1:T(8,128)(2,1)S(1)} %get-tuple-element.1186), channel_id=1, source_target_pairs={{0,2},{2,4},{4,6},{6,8},{8,10},{10,12},{12,14},{14,16},{16,18},{18... | collective-permute-start | bytes 786440 | tf_op jit(solution)/shard_map/while/body/eval_jaxpr/ppermute | solution.py:15
  53.4 2.5 tile.79
  55.9 2.2 slice.180
  58.1 4.6 %reshape.315 = f32[16,128,254]{2,1,0:T(8,128)} reshape(f32[16,32512]{1,0:T(8,128)S(1)} %slice.180) | data formatting | bytes 4161536 | tf_op jit(solution)/shard_map/while/body/eval_jaxpr/reshape | solution.py:51
  69.8 3.2 %collective-permute-start = (bf16[128,1024]{0,1:T(8,128)(2,1)S(1)}, bf16[128,1024]{0,1:T(8,128)(2,1)S(1)}, u32[]{:S(2)}, u32[]{:S(2)}) collective-permute-start(bf16[128,1024]{0,1:T(8,128)(2,1)S(1)} %get-tuple-element.1186), channel_id=1, source_target_pairs={{0,2},{2,4},{4,6},{6,8},{8,10},{10,12},{12,14},{14,16},{16,18},{18... | collective-permute-start | bytes 786440 | tf_op jit(solution)/shard_map/while/body/eval_jaxpr/ppermute | solution.py:15
  75.7 2.5 tile.79
  78.2 2.2 slice.180
  80.3 4.6 %reshape.315 = f32[16,128,254]{2,1,0:T(8,128)} reshape(f32[16,32512]{1,0:T(8,128)S(1)} %slice.180) | data formatting | bytes 4161536 | tf_op jit(solution)/shard_map/while/body/eval_jaxpr/reshape | solution.py:51
  94.5 2.5 tile.69
  97.0 2.2 slice.165
  99.2 4.6 %reshape.298 = f32[16,128,254]{2,1,0:T(8,128)} reshape(f32[16,32512]{1,0:T(8,128)S(1)} %slice.165) | data formatting | bytes 4161536 | tf_op jit(solution)/shard_map/reshape | solution.py:51
  112.8 2.2 fusion.41
  118.7 4.8 %reshape.301 = f32[16,128,255]{2,1,0:T(8,128)S(1)} reshape(f32[16,32640]{1,0:T(8,128)} %slice.167) | data formatting | bytes 4177920 | tf_op jit(solution)/shard_map/reshape | solution.py:42
  123.9 109.7 %while.53 = (s32[]{:T(128)}, f32[128,1024]{0,1:T(8,128)}, f32[128,1024]{0,1:T(8,128)}, f32[128,1024]{0,1:T(8,128)}, f32[16,128]{1,0:T(8,128)S(1)}, /*index=5*/bf...) while((s32[]{:T(128)}, f32[128,1024]{0,1:T(8,128)}, ...), condition=%wide.region_11.12_spmd.clone, body=%wide.region_9.11_spmd.clone.sunk | while | flops 183988240 | bytes 71119040 | solution.py:157
  124.0 2.4 collective-permute-start.2
  126.5 1.9 collective-permute-start.3
  129.1 2.5 tile.81
  131.6 2.2 slice.183
  133.8 4.6 %reshape.316 = f32[16,128,254]{2,1,0:T(8,128)} reshape(f32[16,32512]{1,0:T(8,128)S(1)} %slice.183) | data formatting | bytes 4161536 | tf_op jit(solution)/shard_map/while/body/eval_jaxpr/reshape | solution.py:51
  150.0 4.8 %reshape.317 = f32[16,128,255]{2,1,0:T(8,128)S(1)} reshape(f32[16,32640]{1,0:T(8,128)} %slice.185) | data formatting | bytes 4177920 | tf_op jit(solution)/shard_map/while/body/eval_jaxpr/reshape | solution.py:42
  156.9 2.1 bitcast_add_fusion.7
  162.8 1.9 collective-permute-start.3
  165.4 2.5 tile.81
  167.9 2.2 slice.183
  170.1 4.6 %reshape.316 = f32[16,128,254]{2,1,0:T(8,128)} reshape(f32[16,32512]{1,0:T(8,128)S(1)} %slice.183) | data formatting | bytes 4161536 | tf_op jit(solution)/shard_map/while/body/eval_jaxpr/reshape | solution.py:51
  186.3 4.8 %reshape.317 = f32[16,128,255]{2,1,0:T(8,128)S(1)} reshape(f32[16,32640]{1,0:T(8,128)} %slice.185) | data formatting | bytes 4177920 | tf_op jit(solution)/shard_map/while/body/eval_jaxpr/reshape | solution.py:42
  193.2 2.1 bitcast_add_fusion.7
  199.1 1.9 collective-permute-start.3
  201.7 2.5 tile.81
  204.2 2.2 slice.183
  206.4 4.6 %reshape.316 = f32[16,128,254]{2,1,0:T(8,128)} reshape(f32[16,32512]{1,0:T(8,128)S(1)} %slice.183) | data formatting | bytes 4161536 | tf_op jit(solution)/shard_map/while/body/eval_jaxpr/reshape | solution.py:51
  222.6 4.8 %reshape.317 = f32[16,128,255]{2,1,0:T(8,128)S(1)} reshape(f32[16,32640]{1,0:T(8,128)} %slice.185) | data formatting | bytes 4177920 | tf_op jit(solution)/shard_map/while/body/eval_jaxpr/reshape | solution.py:42
  229.6 2.1 bitcast_add_fusion.7
  233.5 17.0 %psum.28 = f32[16,128]{1,0:T(8,128)S(1)} all-reduce(f32[16,128]{1,0:T(8,128)S(1)} %get-tuple-element.814), channel_id=1, replica_groups=mesh['seq_0'=4,'seq_1'=4,'seq_2'=4,'seq_3'=2,'head'=2] {'seq_0'}, use_global_device_ids=true, to_apply=%region_12.13 | all-reduce | flops 2048 | bytes 16384 | tf_op jit(solution)/shard_map/psum | solution.py:19
  250.5 6.7 %psum.29 = f32[16,128]{1,0:T(8,128)S(1)} all-reduce(f32[16,128]{1,0:T(8,128)S(1)} %psum.28), channel_id=1, replica_groups=mesh['seq_0'=4,'seq_1'=4,'seq_2'=4,'seq_3'=2,'head'=2] {'seq_1'}, use_global_device_ids=true, to_apply=%region_13.14 | all-reduce | flops 2048 | bytes 16384 | tf_op jit(solution)/shard_map/psum | solution.py:19
  257.3 7.3 %psum.30 = f32[16,128]{1,0:T(8,128)S(1)} all-reduce(f32[16,128]{1,0:T(8,128)S(1)} %psum.29), channel_id=1, replica_groups=mesh['seq_0'=4,'seq_1'=4,'seq_2'=4,'seq_3'=2,'head'=2] {'seq_2'}, use_global_device_ids=true, to_apply=%region_14.15 | all-reduce | flops 2048 | bytes 16384 | tf_op jit(solution)/shard_map/psum | solution.py:19
  264.6 8.8 %psum.31 = f32[16,128]{1,0:T(8,128)S(1)} all-reduce(f32[16,128]{1,0:T(8,128)S(1)} %psum.30), channel_id=1, replica_groups=mesh['seq_0'=4,'seq_1'=4,'seq_2'=4,'seq_3'=2,'head'=2] {'seq_3'}, use_global_device_ids=true, to_apply=%region_15.16 | all-reduce | flops 2048 | bytes 16384 | tf_op jit(solution)/shard_map/psum | solution.py:19
  274.0 5.4 %all-to-all-start = ((f32[2,16,128]{2,1,0:T(8,128)}), f32[2,16,128]{2,1,0:T(8,128)S(1)}, u32[]{:S(2)}, u32[]{:S(2)}) async-start(f32[2,16,128]{2,1,0:T(8,128)} %broadcast_in_dim.186), calls=%async_computation | async-start | bytes 32768 | tf_op jit(solution)/shard_map/all_to_all | solution.py:30
  (236 shorter events, 109.6 us)
Async XLA Ops:
  14.9 1.2 slice-start.2
  14.9 1.6 copy-start.6
  16.5 1.0 copy-start.7
  17.1 4.4 %copy-start.10 = (s32[1,4]{1,0:T(1,128)S(1)}, s32[1,4]{1,0:T(1,128)}, u32[]{:S(2)}) copy-start(s32[1,4]{1,0:T(1,128)} %param.21) | copy-start | bytes 52
  19.4 4.4 %copy-start.8 = (s32[1,4,256]{2,1,0:T(4,128)S(1)}, s32[1,4,256]{2,1,0:T(4,128)}, u32[]{:S(2)}) copy-start(s32[1,4,256]{2,1,0:T(4,128)} %param.20) | copy-start | bytes 12292
  19.4 4.4 %copy-start.9 = (f32[16,128]{1,0:T(8,128)S(1)}, f32[16,128]{1,0:T(8,128)}, u32[]{:S(2)}) copy-start(f32[16,128]{1,0:T(8,128)} %param.19) | copy-start | bytes 24580
  23.8 19.3 %collective-permute-start = (bf16[128,1024]{0,1:T(8,128)(2,1)S(1)}, bf16[128,1024]{0,1:T(8,128)(2,1)S(1)}, u32[]{:S(2)}, u32[]{:S(2)}) collective-permute-start(bf16[128,1024]{0,1:T(8,128)(2,1)S(1)} %get-tuple-element.1186), channel_id=1, source_target_pairs={{0,2},{2,4},{4,6},{6,8},{8,10},{10,12},{12,14},{14,16},{16,18},{18... | collective-permute-start | bytes 786440 | tf_op jit(solution)/shard_map/while/body/eval_jaxpr/ppermute | solution.py:15
  28.3 15.4 %collective-permute-start.1 = (bf16[128,1024]{0,1:T(8,128)(2,1)}, bf16[128,1024]{0,1:T(8,128)(2,1)S(1)}, u32[]{:S(2)}, u32[]{:S(2)}) collective-permute-start(bf16[128,1024]{0,1:T(8,128)(2,1)} %get-tuple-element.1187), channel_id=1, source_target_pairs={{0,2},{2,4},{4,6},{6,8},{8,10},{10,12},{12,14},{14,16},{16,18},{18... | collective-permute-start | bytes 786440 | tf_op jit(solution)/shard_map/while/body/eval_jaxpr/ppermute | solution.py:15
  40.2 1.2 slice-start
  47.3 18.3 %collective-permute-start = (bf16[128,1024]{0,1:T(8,128)(2,1)S(1)}, bf16[128,1024]{0,1:T(8,128)(2,1)S(1)}, u32[]{:S(2)}, u32[]{:S(2)}) collective-permute-start(bf16[128,1024]{0,1:T(8,128)(2,1)S(1)} %get-tuple-element.1186), channel_id=1, source_target_pairs={{0,2},{2,4},{4,6},{6,8},{8,10},{10,12},{12,14},{14,16},{16,18},{18... | collective-permute-start | bytes 786440 | tf_op jit(solution)/shard_map/while/body/eval_jaxpr/ppermute | solution.py:15
  50.8 15.4 %collective-permute-start.1 = (bf16[128,1024]{0,1:T(8,128)(2,1)}, bf16[128,1024]{0,1:T(8,128)(2,1)S(1)}, u32[]{:S(2)}, u32[]{:S(2)}) collective-permute-start(bf16[128,1024]{0,1:T(8,128)(2,1)} %get-tuple-element.1187), channel_id=1, source_target_pairs={{0,2},{2,4},{4,6},{6,8},{8,10},{10,12},{12,14},{14,16},{16,18},{18... | collective-permute-start | bytes 786440 | tf_op jit(solution)/shard_map/while/body/eval_jaxpr/ppermute | solution.py:15
  62.7 1.2 slice-start
  69.8 18.0 %collective-permute-start = (bf16[128,1024]{0,1:T(8,128)(2,1)S(1)}, bf16[128,1024]{0,1:T(8,128)(2,1)S(1)}, u32[]{:S(2)}, u32[]{:S(2)}) collective-permute-start(bf16[128,1024]{0,1:T(8,128)(2,1)S(1)} %get-tuple-element.1186), channel_id=1, source_target_pairs={{0,2},{2,4},{4,6},{6,8},{8,10},{10,12},{12,14},{14,16},{16,18},{18... | collective-permute-start | bytes 786440 | tf_op jit(solution)/shard_map/while/body/eval_jaxpr/ppermute | solution.py:15
  73.1 15.4 %collective-permute-start.1 = (bf16[128,1024]{0,1:T(8,128)(2,1)}, bf16[128,1024]{0,1:T(8,128)(2,1)S(1)}, u32[]{:S(2)}, u32[]{:S(2)}) collective-permute-start(bf16[128,1024]{0,1:T(8,128)(2,1)} %get-tuple-element.1187), channel_id=1, source_target_pairs={{0,2},{2,4},{4,6},{6,8},{8,10},{10,12},{12,14},{14,16},{16,18},{18... | collective-permute-start | bytes 786440 | tf_op jit(solution)/shard_map/while/body/eval_jaxpr/ppermute | solution.py:15
  84.9 1.2 slice-start
  103.7 1.2 slice-start.3
  107.6 1.5 copy-start.5
  107.6 2.8 copy-start.4
  124.0 32.9 %collective-permute-start.2 = (f32[128,1024]{0,1:T(8,128)}, f32[128,1024]{0,1:T(8,128)}, u32[]{:S(2)}, u32[]{:S(2)}) collective-permute-start(f32[128,1024]{0,1:T(8,128)} %get-tuple-element.1244), channel_id=1, source_target_pairs={{2,0},{4,2},{6,4},{8,6},{10,8},{12,10},{14,12},{16,14},{18,16},{20... | collective-permute-start | bytes 1572872 | tf_op jit(solution)/shard_map/while/body/eval_jaxpr/ppermute | solution.py:15
  126.5 32.5 %collective-permute-start.3 = (f32[128,1024]{0,1:T(8,128)}, f32[128,1024]{0,1:T(8,128)}, u32[]{:S(2)}, u32[]{:S(2)}) collective-permute-start(f32[128,1024]{0,1:T(8,128)} %get-tuple-element.1245), channel_id=1, source_target_pairs={{2,0},{4,2},{6,4},{8,6},{10,8},{12,10},{14,12},{16,14},{18,16},{20... | collective-permute-start | bytes 1572872 | tf_op jit(solution)/shard_map/while/body/eval_jaxpr/ppermute | solution.py:15
  138.3 1.2 slice-start.1
  155.0 1.8 copy-start.1
  155.0 1.8 copy-start.2
  155.0 1.9 copy-start
  156.9 4.0 %copy-start.3 = (f32[128,1024]{0,1:T(8,128)}, f32[128,1024]{0,1:T(8,128)S(1)}, u32[]{:S(2)}) copy-start(f32[128,1024]{0,1:T(8,128)S(1)} %bitcast_add_fusion.6) | copy-start | bytes 1572868 | tf_op jit(solution)/shard_map/while
  160.9 32.3 %collective-permute-start.2 = (f32[128,1024]{0,1:T(8,128)}, f32[128,1024]{0,1:T(8,128)}, u32[]{:S(2)}, u32[]{:S(2)}) collective-permute-start(f32[128,1024]{0,1:T(8,128)} %get-tuple-element.1244), channel_id=1, source_target_pairs={{2,0},{4,2},{6,4},{8,6},{10,8},{12,10},{14,12},{16,14},{18,16},{20... | collective-permute-start | bytes 1572872 | tf_op jit(solution)/shard_map/while/body/eval_jaxpr/ppermute | solution.py:15
  162.8 32.5 %collective-permute-start.3 = (f32[128,1024]{0,1:T(8,128)}, f32[128,1024]{0,1:T(8,128)}, u32[]{:S(2)}, u32[]{:S(2)}) collective-permute-start(f32[128,1024]{0,1:T(8,128)} %get-tuple-element.1245), channel_id=1, source_target_pairs={{2,0},{4,2},{6,4},{8,6},{10,8},{12,10},{14,12},{16,14},{18,16},{20... | collective-permute-start | bytes 1572872 | tf_op jit(solution)/shard_map/while/body/eval_jaxpr/ppermute | solution.py:15
  174.7 1.2 slice-start.1
  191.3 1.8 copy-start.1
  191.3 1.8 copy-start.2
  191.3 1.9 copy-start
  193.2 4.0 %copy-start.3 = (f32[128,1024]{0,1:T(8,128)}, f32[128,1024]{0,1:T(8,128)S(1)}, u32[]{:S(2)}) copy-start(f32[128,1024]{0,1:T(8,128)S(1)} %bitcast_add_fusion.6) | copy-start | bytes 1572868 | tf_op jit(solution)/shard_map/while
  197.2 32.3 %collective-permute-start.2 = (f32[128,1024]{0,1:T(8,128)}, f32[128,1024]{0,1:T(8,128)}, u32[]{:S(2)}, u32[]{:S(2)}) collective-permute-start(f32[128,1024]{0,1:T(8,128)} %get-tuple-element.1244), channel_id=1, source_target_pairs={{2,0},{4,2},{6,4},{8,6},{10,8},{12,10},{14,12},{16,14},{18,16},{20... | collective-permute-start | bytes 1572872 | tf_op jit(solution)/shard_map/while/body/eval_jaxpr/ppermute | solution.py:15
  199.1 32.5 %collective-permute-start.3 = (f32[128,1024]{0,1:T(8,128)}, f32[128,1024]{0,1:T(8,128)}, u32[]{:S(2)}, u32[]{:S(2)}) collective-permute-start(f32[128,1024]{0,1:T(8,128)} %get-tuple-element.1245), channel_id=1, source_target_pairs={{2,0},{4,2},{6,4},{8,6},{10,8},{12,10},{14,12},{16,14},{18,16},{20... | collective-permute-start | bytes 1572872 | tf_op jit(solution)/shard_map/while/body/eval_jaxpr/ppermute | solution.py:15
  211.0 1.2 slice-start.1
  227.6 1.8 copy-start.1
  227.6 1.8 copy-start.2
  227.7 1.9 copy-start
  229.5 4.0 %copy-start.3 = (f32[128,1024]{0,1:T(8,128)}, f32[128,1024]{0,1:T(8,128)S(1)}, u32[]{:S(2)}) copy-start(f32[128,1024]{0,1:T(8,128)S(1)} %bitcast_add_fusion.6) | copy-start | bytes 1572868 | tf_op jit(solution)/shard_map/while
  274.0 12.0 %all-to-all-start = ((f32[2,16,128]{2,1,0:T(8,128)}), f32[2,16,128]{2,1,0:T(8,128)S(1)}, u32[]{:S(2)}, u32[]{:S(2)}) async-start(f32[2,16,128]{2,1,0:T(8,128)} %broadcast_in_dim.186), calls=%async_computation | async-start | bytes 32768 | tf_op jit(solution)/shard_map/all_to_all | solution.py:30
where the time goes:
time: 289 us; the launch traced here: 287 us
  local copies, waits for them, and re-layouts  156 us (54%)
  blocking collectives  39.8 us (14%)
  matrix products  34.5 us (12%)
  starting transfers between devices  34.4 us (12%)
  other arithmetic  13.8 us (5%)
  loops' own time  5.23 us (2%)
    psum x4, blocking collectives, over_axes(): return functools.reduce(lax.psum, axes, value)  39.8 us
    reshape x8, local copies, waits for them, and re-layouts, toeplitz_rows(): return window.reshape(heads, rows, 2 * rows - 2)[:, :, :rows]  36.5 us
    ppermute x12, starting transfers between devices, passed_along(): return lax.ppermute(value, axis, pairs)  29 us
    another operation x16, local copies, waits for them, and re-layouts, toeplitz_rows(): tiled = jnp.tile(reverse, (1, rows))  21.3 us
    reshape x4, local copies, waits for them, and re-layouts, diagonal_sums(): sums = sheared.reshape(heads, rows, 2 * rows - 1).sum(axis=1)  19.2 us
    slice x8, local copies, waits for them, and re-layouts, toeplitz_rows(): window = tiled[:, rows - 1:rows - 1 + rows * (2 * rows - 2)]  17.5 us
    dot_general x8, matrix products, pair_terms(): jnp.einsum('qhd,khd->hqk', cot_heads, value_heads, preferred_element_type...  10.8 us
    while x57, local copies, waits for them, and re-layouts  10.6 us
  transfers between devices with their start and end apart: 13, of which 1 were waited for; matrix products, arithmetic and copies ran while one was open for 44% of the time, Pallas kernels for 0%

commit v1 on v0

v1 whole, which is shorter than its diff:
```python
import functools

import jax
import jax.numpy as jnp
from jax import lax
from jax.experimental import pallas as pl
from jax.experimental.pallas import tpu as pltpu
from jax.sharding import PartitionSpec as P

MESH = pl.DeviceIdType.MESH
LOG2E = 1.4426950408889634
NEG = -1e30
F32 = jnp.float32
BF16 = jnp.bfloat16
AHEAD = 3
NT = (((1,), (1,)), ((), ()))


def dot_nt(a, b, **kw):
    return lax.dot_general(a, b, NT, preferred_element_type=F32, **kw)


def dot_nn(a, b, **kw):
    return jnp.dot(a, b, preferred_element_type=F32, **kw)


def kernel(
    sizes,
    q_hbm, k_hbm, v_hbm, do_hbm, table_hbm, ids_hbm, mask_hbm,
    dq_ref, dk_ref, dv_ref, gb_ref,
    kv, qd, tableb, idsb, maskb, byb, biasq, biask,
    ss, sp, dsb, pb, ks, kp, kpb, kdsb, dk0b, dv0b, st, dgb,
    xpart, xbuf, ybuf, zbuf,
    load_sem, small_sem, kv_send, kv_recv, qd_send, qd_recv,
    st_send, st_recv, id_send, id_recv,
    xs_sem, xr_sem, ys_sem, yr_sem, zs_sem, zr_sem,
):
    n_seq, nx, ny, nz, n_head, heads, groups = sizes
    T, W = 128, 128
    scale = 0.125
    c = scale * LOG2E
    me = lax.axis_index("seq")
    hi = lax.axis_index("head")
    core = lax.rem(me, 2)
    partner = me + 1 - 2 * core

    def at(offset):
        return lax.rem(me + (offset + n_seq), n_seq)

    row = 2 * nx
    in_row = lax.rem(me, row)
    row_base = me - in_row
    y_at = lax.rem(me // row, ny)
    z_at = me // (row * ny)
    in_plane = lax.rem(me, row * ny)
    halves = heads // 2
    ring_z = n_head * nz * 2
    in_z = (hi * nz + z_at) * 2 + core

    def x_partner(t):
        return row_base + lax.rem(in_row + t, row)

    def y_partner(t):
        return z_at * (row * ny) + lax.rem(y_at + t, ny) * row + in_row

    def z_partner(t):
        w = lax.rem(in_z + t, ring_z)
        w_core = lax.rem(w, 2)
        w_z = lax.rem(w // 2, nz)
        w_head = w // (2 * nz)
        return {"seq": w_z * (row * ny) + in_plane - core + w_core, "head": w_head}

    srcs = ((q_hbm, qd, 0), (do_hbm, qd, W), (k_hbm, kv, 0), (v_hbm, kv, W))

    def load(n, g):
        src, dst, off = srcs[n]
        return pltpu.make_async_copy(
            src.at[:, pl.ds(g * W, W)], dst.at[g, pl.ds(0, T), pl.ds(off, W)], load_sem.at[n, g]
        )

    for g in range(groups):
        for n in (2, 3, 0, 1):
            load(n, g).start()
    small = [
        pltpu.make_async_copy(table_hbm, tableb, small_sem.at[0]),
        pltpu.make_async_copy(ids_hbm.at[0], idsb.at[0], small_sem.at[1]),
        pltpu.make_async_copy(mask_hbm, maskb.at[0], small_sem.at[2]),
    ]
    for copy in small:
        copy.start()

    barrier = pltpu.get_barrier_semaphore()
    partners = [{"seq": at(o)} for o in (1, 2, 3, -1, -2, -3)]
    partners += [{"seq": x_partner(t)} for t in range(1, row)]
    partners += [{"seq": y_partner(t)} for t in range(1, ny)]
    partners += [z_partner(t) for t in range(1, ring_z)]
    for other in partners:
        pl.semaphore_signal(barrier, inc=1, device_id=other, device_id_type=MESH)

    def remote(src, dst, send, recv, device):
        return pltpu.make_async_remote_copy(
            src_ref=src, dst_ref=dst, send_sem=send, recv_sem=recv, device_id=device, device_id_type=MESH
        )

    def slot(buf, g, s):
        return buf.at[g, pl.ds(s * T, T)]

    def kv_copy(n, g):
        if n == 0:
            src, s, device = slot(kv, g, 0), 2, at(2)
        elif n == 1:
            src, s, device = slot(kv, g, 2), 3, at(1)
        else:
            src, s, device = slot(kv, g, pl.multiple_of(2 * core, 2)), 1, partner
        return remote(src, slot(kv, g, s), kv_send.at[n, g], kv_recv.at[s - 1, g], {"seq": device})

    def qd_copy(n, g):
        if n == 0:
            src, s, device = slot(qd, g, 0), 2, at(-2)
        elif n == 1:
            src, s, device = slot(qd, g, 2), 3, at(-1)
        else:
            src, s, device = slot(qd, g, pl.multiple_of(2 - 2 * core, 2)), 1, partner
        return remote(src, slot(qd, g, s), qd_send.at[n, g], qd_recv.at[s - 1, g], {"seq": device})

    by_slot = {1: 2, 2: 0, 3: 1}

    def kv_arrived(s, g):
        kv_copy(by_slot[s], g).wait_recv()

    def qd_arrived(s, g):
        qd_copy(by_slot[s], g).wait_recv()

    def st_copy(s, g):
        return remote(st.at[0, g], st.at[s, g], st_send.at[s - 1, g], st_recv.at[s - 1, g], {"seq": at(-s)})

    def id_copy(s):
        return remote(idsb.at[0], idsb.at[s], id_send.at[0, s - 1], id_recv.at[0, s - 1], {"seq": at(-s)})

    def mask_copy(s):
        return remote(maskb.at[0], maskb.at[s], id_send.at[1, s - 1], id_recv.at[1, s - 1], {"seq": at(-s)})

    def send_own(g):
        kv_copy(0, g).start()
        qd_copy(0, g).start()

    for copy in small:
        copy.wait()
    for g in range(groups):
        for n in (2, 3, 0, 1):
            load(n, g).wait()
    pl.semaphore_wait(barrier, len(partners))
    for g in range(AHEAD):
        send_own(g)
    for s in (1, 2, 3):
        id_copy(s).start()
        mask_copy(s).start()

    lane = lax.broadcasted_iota(jnp.int32, (T, T), 1)
    first = lane < 64
    lane8 = lax.broadcasted_iota(jnp.int32, (8, T), 1)
    sub8 = lax.broadcasted_iota(jnp.int32, (8, T), 0)
    codes = lax.broadcasted_iota(jnp.int32, (T, 2 * T), 0)

    def onehot(place, s):
        return (codes == idsb[place, s : s + 1, :]).astype(F32)

    def by_offset(place, s, inside):
        by = dot_nn(tableb[...] * LOG2E, onehot(place, s), precision=lax.Precision.HIGHEST)
        if s:
            keep = jnp.logical_and(maskb[place, 0:1, s : s + 1] == 1, inside)
            by = jnp.where(keep, by, NEG)
        return pltpu.roll(by, 1, 1)

    def skewed(index, head):
        line = jnp.broadcast_to(byb[index, pl.ds(head, 1), :], (8, 2 * T))
        base = pltpu.roll(line, 0, 1, stride=1, stride_axis=0)
        return base[:, :T], base[:, T:]

    def block_row(low, high, a):
        mixed = jnp.where(lane8 >= T - 8 * a, low, high)
        return pltpu.roll(mixed, 8 * a, 1) if a else mixed

    for s in range(4):
        byb[s] = by_offset(0, s, me >= s)

    def build_query(g, carry):
        for h in range(2):
            for s in range(4):
                low, high = skewed(s, 2 * g + h)
                for a in range(16):
                    x = block_row(low, high, a)
                    if s == 0:
                        x = jnp.where(8 * a + sub8 <= lane8, x, NEG)
                    biasq[g, pl.ds(s * T + 8 * a, 8), pl.ds(h * T, T)] = x
        return carry

    lax.fori_loop(0, groups, build_query, 0)
    for s in (1, 2, 3):
        id_copy(s).wait_recv()
        mask_copy(s).wait_recv()
        byb[3 + s] = by_offset(s, s, me + s < n_seq)

    def build_key(g, carry):
        for h in range(2):
            for s in (1, 2, 3):
                low, high = skewed(3 + s, 2 * g + h)
                for a in range(16):
                    biask[g, pl.ds(h * T + 8 * a, 8), pl.ds((s - 1) * T, T)] = block_row(low, high, a)
        return carry

    lax.fori_loop(0, groups, build_key, 0)

    def two(x):
        zero = jnp.zeros_like(x)
        return jnp.concatenate([jnp.where(first, x, zero), jnp.where(first, zero, x)], axis=0)

    def merged(x):
        return jnp.where(first, x[:T], x[T:])

    R = 32

    def fold(x, op):
        parts = [x[8 * j : 8 * j + 8] for j in range(x.shape[0] // 8)]
        return functools.reduce(op, parts)

    def query_side(g):
        q2, do2 = qd[g, 0:T, 0:W], qd[g, 0:T, W : 2 * W]
        ss[...] = dot_nt(kv[g, :, 0:W], two(q2))
        sp[...] = dot_nt(kv[g, :, W : 2 * W], two(do2))
        top = jnp.full((8, 2 * T), NEG, F32)
        for r in range(0, 4 * T, R):
            x = ss[r : r + R] * c + biasq[g, r : r + R]
            ss[r : r + R] = x
            top = jnp.maximum(top, fold(x, jnp.maximum))
        top = top.max(axis=0, keepdims=True)
        total = jnp.zeros((8, 2 * T), F32)
        accum = jnp.zeros((8, 2 * T), F32)
        for r in range(0, 4 * T, R):
            e = jnp.exp2(ss[r : r + R] - top)
            ss[r : r + R] = e
            total = total + fold(e, jnp.add)
            accum = accum + fold(e * sp[r : r + R], jnp.add)
        total = total.sum(axis=0, keepdims=True)
        accum = accum.sum(axis=0, keepdims=True)
        inverse = 1.0 / total
        delta = accum / total
        lse = top + jnp.log2(total)
        st[0, g, 0:1, :] = lse[:, :T]
        st[0, g, 1:2, :] = lse[:, T:]
        st[0, g, 2:3, :] = delta[:, :T]
        st[0, g, 3:4, :] = delta[:, T:]
        for s in range(4):
            low = [jnp.zeros((8, T), F32) for _ in range(2)]
            high = [jnp.zeros((8, T), F32) for _ in range(2)]
            for r in range(s * T, s * T + T, R):
                p = ss[r : r + R] * inverse
                ds = p * (sp[r : r + R] - delta)
                dsb[r : r + R] = ds.astype(BF16)
                if s == 0:
                    pb[r : r + R] = p.astype(BF16)
                for j in range(R // 8):
                    a = (r - s * T) // 8 + j
                    for h in range(2):
                        x = ds[8 * j : 8 * j + 8, h * T : h * T + T]
                        if a:
                            x = pltpu.roll(x, T - 8 * a, 1)
                            here = lane8 < T - 8 * a
                            high[h] = high[h] + jnp.where(here, x, 0.0)
                            low[h] = low[h] + jnp.where(here, 0.0, x)
                        else:
                            high[h] = high[h] + x
            for h in range(2):
                both = jnp.concatenate([low[h], high[h]], axis=1)
                for by in (1, 2, 4):
                    both = both + pltpu.roll(pltpu.roll(both, 2 * T - by, 1), 8 - by, 0)
                dgb[s, pl.ds(2 * g + h, 1), :] = both[0:1]
        turned = dot_nn(kv[g, :, 0:W].T, dsb[...])
        joined = jnp.concatenate([turned[0:64, 0:T], turned[64:T, T : 2 * T]], axis=0)
        dq_ref[:, pl.ds(g * W, W)] = (joined.T * scale).astype(BF16)
        for s in (1, 2, 3):
            st_copy(s, g).start()
        dv0b[g] = jnp.where(first, dot_nn(pb[:, 0:T], do2), dot_nn(pb[:, T : 2 * T], do2))
        dk0b[g] = jnp.where(first, dot_nn(dsb[0:T, 0:T], q2), dot_nn(dsb[0:T, T : 2 * T], q2))

    def key_side(g):
        qs, dos = qd[g, T : 4 * T, 0:W], qd[g, T : 4 * T, W : 2 * W]
        ks[...] = dot_nt(two(kv[g, 0:T, 0:W]), qs)
        kp[...] = dot_nt(two(kv[g, 0:T, W : 2 * W]), dos)
        for h in range(2):
            for s in (1, 2, 3):
                lse = st[s, g, h : h + 1, :]
                delta = st[s, g, 2 + h : 3 + h, :]
                cols = slice((s - 1) * T, s * T)
                for r in range(h * T, h * T + T, R):
                    x = ks[r : r + R, cols] * c + biask[g, r : r + R, cols]
                    p = jnp.exp2(x - lse)
                    ds = p * (kp[r : r + R, cols] - delta)
                    kpb[r : r + R, cols] = p.astype(BF16)
                    kdsb[r : r + R, cols] = ds.astype(BF16)
        dv_ref[:, pl.ds(g * W, W)] = (merged(dot_nn(kpb[...], dos)) + dv0b[g]).astype(BF16)
        dk_ref[:, pl.ds(g * W, W)] = ((merged(dot_nn(kdsb[...], qs)) + dk0b[g]) * scale).astype(BF16)

    def key_ready(g):
        for s in (1, 3):
            qd_arrived(s, g)
        for s in (1, 2, 3):
            st_copy(s, g).wait_recv()

    def step(g, carry):
        kv_arrived(2, g)
        kv_copy(1, g).start()
        kv_copy(2, g).start()
        qd_arrived(2, g)
        qd_copy(1, g).start()
        qd_copy(2, g).start()

        @pl.when(g + AHEAD < groups)
        def _():
            send_own(g + AHEAD)

        kv_arrived(3, g)
        kv_arrived(1, g)
        query_side(g)

        @pl.when(g > 0)
        def _():
            key_ready(g - 1)
            key_side(g - 1)

        return carry

    lax.fori_loop(0, groups, step, 0)

    part = jnp.zeros((heads, T), F32)
    for s in range(4):
        part = part + dot_nt(pltpu.roll(dgb[s], 2 * T - 1, 1), onehot(0, s), precision=lax.Precision.HIGHEST)
    xpart[...] = part

    def x_copy(t):
        other = x_partner(t)
        half = pl.multiple_of(lax.rem(other, 2) * halves, halves)
        return remote(xpart.at[pl.ds(half, halves)], xbuf.at[in_row], xs_sem.at[t - 1], xr_sem.at[t - 1], {"seq": other})

    def y_copy(t):
        return remote(ybuf.at[y_at], ybuf.at[y_at], ys_sem.at[t - 1], yr_sem.at[t - 1], {"seq": y_partner(t)})

    def z_copy(t):
        return remote(zbuf.at[in_z], zbuf.at[in_z], zs_sem.at[t - 1], zr_sem.at[t - 1], z_partner(t))

    def total_of(buf, slots):
        return functools.reduce(jnp.add, [buf[i] for i in slots])

    for t in range(1, row):
        x_copy(t).start()
    xbuf[in_row] = xpart[pl.ds(pl.multiple_of(core * halves, halves), halves), :]
    key_ready(groups - 1)
    key_side(groups - 1)
    for t in range(1, row):
        x_copy(t).wait_recv()
    ybuf[y_at] = total_of(xbuf, range(row))
    for t in range(1, ny):
        y_copy(t).start()
    for t in range(1, ny):
        y_copy(t).wait_recv()
    zbuf[in_z] = total_of(ybuf, range(ny))
    for t in range(1, ring_z):
        z_copy(t).start()
    for t in range(1, ring_z):
        z_copy(t).wait_recv()
    for h in range(n_head):
        for half in range(2):
            gb_ref[h * heads + half * halves : h * heads + (half + 1) * halves] = total_of(
                zbuf, [(h * nz + z) * 2 + half for z in range(nz)]
            )

    def drain(g, carry):
        for n in range(3):
            kv_copy(n, g).wait_send()
            qd_copy(n, g).wait_send()
        for s in (1, 2, 3):
            st_copy(s, g).wait_send()
        return carry

    lax.fori_loop(0, groups, drain, 0)
    for s in (1, 2, 3):
        id_copy(s).wait_send()
        mask_copy(s).wait_send()
    for t in range(1, row):
        x_copy(t).wait_send()
    for t in range(1, ny):
        y_copy(t).wait_send()
    for t in range(1, ring_z):
        z_copy(t).wait_send()


def solution(mesh):
    n_seq, n_head = mesh.shape["seq"], mesh.shape["head"]
    nx, ny, nz = (4, 4, 4) if n_seq == 128 else (2, 1, 2)

    def body(queries, keys, values, grad_out, bias_table, bucket_ids, block_mask):
        tok, width = queries.shape
        heads, buckets = bias_table.shape
        groups = width // 128
        sizes = (n_seq, nx, ny, nz, n_head, heads, groups)
        row = 2 * nx
        ring_z = n_head * nz * 2
        operands = (queries, keys, values, grad_out, bias_table, bucket_ids, block_mask)
        V = pltpu.VMEM
        dma = pltpu.SemaphoreType.DMA
        scratch = [
            V((groups, 512, 256), BF16), V((groups, 512, 256), BF16),
            V((heads, 128), F32), V((4, 4, 256), jnp.int32), V((4, 1, 4), jnp.int32),
            V((7, heads, 256), F32), V((groups, 512, 256), F32), V((groups, 256, 384), F32),
            V((512, 256), F32), V((512, 256), F32), V((512, 256), BF16), V((128, 256), BF16),
            V((256, 384), F32), V((256, 384), F32), V((256, 384), BF16), V((256, 384), BF16),
            V((groups, 128, 128), F32), V((groups, 128, 128), F32),
            V((4, groups, 8, 128), F32), V((4, heads, 256), F32),
            V((heads, 128), F32), V((row, heads // 2, 128), F32), V((ny, heads // 2, 128), F32),
            V((ring_z, heads // 2, 128), F32),
            dma((4, groups)), dma((3,)),
            dma((3, groups)), dma((3, groups)), dma((3, groups)), dma((3, groups)),
            dma((3, groups)), dma((3, groups)), dma((2, 3)), dma((2, 3)),
            dma((row - 1,)), dma((row - 1,)), dma((max(ny - 1, 1),)), dma((max(ny - 1, 1),)),
            dma((ring_z - 1,)), dma((ring_z - 1,)),
        ]
        in_hbm = pl.BlockSpec(memory_space=pltpu.HBM)
        in_vmem = pl.BlockSpec(memory_space=pltpu.VMEM)
        out = jax.ShapeDtypeStruct((tok, width), BF16)
        return pl.pallas_call(
            functools.partial(kernel, sizes),
            out_shape=(out, out, out, jax.ShapeDtypeStruct((n_head * heads, buckets), F32)),
            in_specs=[in_hbm] * 7,
            out_specs=(in_vmem,) * 4,
            scratch_shapes=scratch,
            compiler_params=pltpu.CompilerParams(
                collective_id=0, has_side_effects=True, vmem_limit_bytes=48 * 1024 * 1024
            ),
        )(*(pltpu.with_memory_space_constraint(x, pltpu.HBM) for x in operands))

    block = P("seq", "head")
    return jax.shard_map(
        body,
        mesh=mesh,
        in_specs=(block, block, block, block, P("head", None), P("seq", None, None), P("seq", None)),
        out_specs=(block, block, block, P(None, None)),
        check_vma=False,
    )
```

time: 289 us -> 91 us (0.31)
  local copies, waits for them, and re-layouts: 156 us -> 2.71 us
  Pallas kernels: 0 us -> 87.5 us
  blocking collectives: 39.8 us -> 0 us
  matrix products: 34.5 us -> 0 us
  starting transfers between devices: 34.4 us -> 0 us
  other arithmetic: 13.8 us -> 0 us
  loops' own time: 5.23 us -> 0 us
    pallas_call x0 -> x1, Pallas kernels: none -> 87.5 us  [body(): pl.pallas_call(functools.partial(kernel, sizes), out_shape=(out, out, out...]
    reshape x12 -> x0, local copies, waits for them, and re-layouts: 55.8 us -> none  [the longest x8 36.5 us: toeplitz_rows(): return window.reshape(heads, rows, 2 * rows - 2)[:, :, :rows]]
    psum x4 -> x0, blocking collectives: 39.8 us -> none  [over_axes(): return functools.reduce(lax.psum, axes, value)]
    slice x30 -> x0, local copies, waits for them, and re-layouts: 36.6 us -> none  [the longest x8 17.5 us: toeplitz_rows(): window = tiled[:, rows - 1:rows - 1 + rows * (2 * rows - 2)]]
    dot_general x40 -> x0, matrix products: 34.5 us -> none  [the longest x8 10.8 us: pair_terms(): jnp.einsum('qhd,khd->hqk', cot_heads, value_heads, preferred_element_type...]
    ppermute x12 -> x0, starting transfers between devices: 29 us -> none  [passed_along(): return lax.ppermute(value, axis, pairs)]
    another operation x16 -> x0, local copies, waits for them, and re-layouts: 21.3 us -> none  [toeplitz_rows(): tiled = jnp.tile(reverse, (1, rows))]
    while x60 -> x0, local copies, waits for them, and re-layouts: 16.2 us -> none
  transfers between devices with their start and end apart: 13 -> 0, of which waited for: 1 -> 0; matrix products, arithmetic and copies ran while one was open for 44% -> 0% of each run, Pallas kernels for 0% -> 0%
where the time goes in v1:
time: 91 us; the launch traced here: 90.8 us
  Pallas kernels  87.5 us (96%)
  local copies, waits for them, and re-layouts  2.71 us (3%)
    pallas_call x1, Pallas kernels, body(): pl.pallas_call(functools.partial(kernel, sizes), out_shape=(out, out, out...  87.5 us
    unnamed x4, local copies, waits for them, and re-layouts  2.71 us

profile of v1, /device:TPU:1, one launch (start us, length us, event | category | flops | bytes accessed | tf_op | source)
XLA Modules:
  0.0 90.8 jit_solution(1262296773511354254)
XLA Ops:
  0.6 87.5 %shard_map.102 = (bf16[128,1024]{1,0:T(8,128)(2,1)S(1)}, bf16[128,1024]{1,0:T(8,128)(2,1)S(1)}, bf16[128,1024]{1,0:T(8,128)(2,1)S(1)}, f32[32,128]{1,0:T(8,128)S(1)}) custom-call(bf16[128,1024]{1,0:T(8,128)(2,1)} %q_hbm.1, bf16[128,1024]{1,0:T(8,128)(2,1)} %k_hbm.1, bf16[128,1024]{1,0:T(8,128)(2,1)} %v_hbm.1, bf16[128,1024]{1,0:T(8,128)(2,1)} %do_hbm.1, ...), custom_call_target="tpu_custom_call" | custom-call | tf_op jit(solution)/shard_map/pallas_call | solution.py:430
  88.1 0.7 copy.15
  88.8 0.7 copy.16
  89.5 0.7 copy.17
  90.2 0.6 copy.18

commit v2 on v1

--- a/solution.py
+++ b/solution.py
@@ -12,7 +12,9 @@
 NEG = -1e30
 F32 = jnp.float32
 BF16 = jnp.bfloat16
-AHEAD = 3
+AHEAD = 5
+RELAY = 2
+LAG = 4
 NT = (((1,), (1,)), ((), ()))
 
 
@@ -123,13 +125,22 @@
             src, s, device = slot(qd, g, pl.multiple_of(2 - 2 * core, 2)), 1, partner
         return remote(src, slot(qd, g, s), qd_send.at[n, g], qd_recv.at[s - 1, g], {"seq": device})
 
+    after = n_seq - 1 - me
+    kv_sent = (after >= 2, jnp.logical_and(me >= 2, after >= 1), jnp.logical_or(core == 0, me >= 2))
+    qd_sent = (me >= 2, jnp.logical_and(after >= 2, me >= 1), jnp.logical_or(core == 1, after >= 2))
     by_slot = {1: 2, 2: 0, 3: 1}
 
+    def kv_start(n, g):
+        pl.when(kv_sent[n])(lambda: kv_copy(n, g).start())
+
+    def qd_start(n, g):
+        pl.when(qd_sent[n])(lambda: qd_copy(n, g).start())
+
     def kv_arrived(s, g):
-        kv_copy(by_slot[s], g).wait_recv()
+        pl.when(me >= s)(lambda: kv_copy(by_slot[s], g).wait_recv())
 
     def qd_arrived(s, g):
-        qd_copy(by_slot[s], g).wait_recv()
+        pl.when(after >= s)(lambda: qd_copy(by_slot[s], g).wait_recv())
 
     def st_copy(s, g):
         return remote(st.at[0, g], st.at[s, g], st_send.at[s - 1, g], st_recv.at[s - 1, g], {"seq": at(-s)})
@@ -141,20 +152,48 @@
         return remote(maskb.at[0], maskb.at[s], id_send.at[1, s - 1], id_recv.at[1, s - 1], {"seq": at(-s)})
 
     def send_own(g):
-        kv_copy(0, g).start()
-        qd_copy(0, g).start()
-
-    for copy in small:
-        copy.wait()
-    for g in range(groups):
-        for n in (2, 3, 0, 1):
-            load(n, g).wait()
-    pl.semaphore_wait(barrier, len(partners))
+        kv_start(0, g)
+        qd_start(0, g)
+
+    def kv_relay(g):
+        kv_arrived(2, g)
+        kv_start(1, g)
+        kv_start(2, g)
+
+    def qd_relay(g):
+        qd_arrived(2, g)
+        qd_start(1, g)
+        qd_start(2, g)
+
+    with jax.named_scope("load_wait"):
+        for copy in small:
+            copy.wait()
+        for g in range(groups):
+            for n in (2, 3, 0, 1):
+                load(n, g).wait()
+    with jax.named_scope("barrier"):
+        pl.semaphore_wait(barrier, len(partners))
+    for s in (1, 2, 3):
+
+        @pl.when(me >= s)
+        def _():
+            id_copy(s).start()
+            mask_copy(s).start()
+
     for g in range(AHEAD):
         send_own(g)
     for s in (1, 2, 3):
-        id_copy(s).start()
-        mask_copy(s).start()
+
+        @pl.when(me < s)
+        def _():
+            kv[:, pl.ds(s * T, T), :] = jnp.zeros((groups, T, 2 * W), BF16)
+
+        @pl.when(after < s)
+        def _():
+            qd[:, pl.ds(s * T, T), :] = jnp.zeros((groups, T, 2 * W), BF16)
+            st[s] = jnp.zeros((groups, 8, T), F32)
+            idsb[s] = jnp.zeros((4, 2 * T), jnp.int32)
+            maskb[s] = jnp.zeros((1, 4), jnp.int32)
 
     lane = lax.broadcasted_iota(jnp.int32, (T, T), 1)
     first = lane < 64
@@ -163,10 +202,20 @@
     codes = lax.broadcasted_iota(jnp.int32, (T, 2 * T), 0)
 
     def onehot(place, s):
-        return (codes == idsb[place, s : s + 1, :]).astype(F32)
+        return (codes == idsb[place, s : s + 1, :]).astype(BF16)
+
+    def thirds(x):
+        big = x.astype(BF16)
+        rest = x - big.astype(F32)
+        mid = rest.astype(BF16)
+        return jnp.concatenate([big, mid, (rest - mid.astype(F32)).astype(BF16)], axis=0)
+
+    def whole(x):
+        n = x.shape[0] // 3
+        return x[:n] + x[n : 2 * n] + x[2 * n :]
 
     def by_offset(place, s, inside):
-        by = dot_nn(tableb[...] * LOG2E, onehot(place, s), precision=lax.Precision.HIGHEST)
+        by = whole(dot_nn(thirds(tableb[...] * LOG2E), onehot(place, s)))
         if s:
             keep = jnp.logical_and(maskb[place, 0:1, s : s + 1] == 1, inside)
             by = jnp.where(keep, by, NEG)
@@ -181,8 +230,9 @@
         mixed = jnp.where(lane8 >= T - 8 * a, low, high)
         return pltpu.roll(mixed, 8 * a, 1) if a else mixed
 
-    for s in range(4):
-        byb[s] = by_offset(0, s, me >= s)
+    with jax.named_scope("by"):
+        for s in range(4):
+            byb[s] = by_offset(0, s, me >= s)
 
     def build_query(g, carry):
         for h in range(2):
@@ -195,11 +245,19 @@
                     biasq[g, pl.ds(s * T + 8 * a, 8), pl.ds(h * T, T)] = x
         return carry
 
-    lax.fori_loop(0, groups, build_query, 0)
-    for s in (1, 2, 3):
-        id_copy(s).wait_recv()
-        mask_copy(s).wait_recv()
-        byb[3 + s] = by_offset(s, s, me + s < n_seq)
+    with jax.named_scope("build_query"):
+        lax.fori_loop(0, groups, build_query, 0)
+    with jax.named_scope("relay_first"):
+        kv_relay(0)
+    with jax.named_scope("by_key"):
+        for s in (1, 2, 3):
+
+            @pl.when(after >= s)
+            def _():
+                id_copy(s).wait_recv()
+                mask_copy(s).wait_recv()
+
+            byb[3 + s] = by_offset(s, s, after >= s)
 
     def build_key(g, carry):
         for h in range(2):
@@ -209,7 +267,11 @@
                     biask[g, pl.ds(h * T + 8 * a, 8), pl.ds((s - 1) * T, T)] = block_row(low, high, a)
         return carry
 
-    lax.fori_loop(0, groups, build_key, 0)
+    with jax.named_scope("build_key"):
+        lax.fori_loop(0, groups, build_key, 0)
+    with jax.named_scope("relay_first"):
+        for g in range(1, RELAY):
+            kv_relay(g)
 
     def two(x):
         zero = jnp.zeros_like(x)
@@ -279,7 +341,7 @@
         joined = jnp.concatenate([turned[0:64, 0:T], turned[64:T, T : 2 * T]], axis=0)
         dq_ref[:, pl.ds(g * W, W)] = (joined.T * scale).astype(BF16)
         for s in (1, 2, 3):
-            st_copy(s, g).start()
+            pl.when(me >= s)(lambda s=s: st_copy(s, g).start())
         dv0b[g] = jnp.where(first, dot_nn(pb[:, 0:T], do2), dot_nn(pb[:, T : 2 * T], do2))
         dk0b[g] = jnp.where(first, dot_nn(dsb[0:T, 0:T], q2), dot_nn(dsb[0:T, T : 2 * T], q2))
 
@@ -305,36 +367,34 @@
         for s in (1, 3):
             qd_arrived(s, g)
         for s in (1, 2, 3):
-            st_copy(s, g).wait_recv()
+            pl.when(after >= s)(lambda s=s: st_copy(s, g).wait_recv())
 
     def step(g, carry):
-        kv_arrived(2, g)
-        kv_copy(1, g).start()
-        kv_copy(2, g).start()
-        qd_arrived(2, g)
-        qd_copy(1, g).start()
-        qd_copy(2, g).start()
-
-        @pl.when(g + AHEAD < groups)
+        with jax.named_scope("relay"):
+            pl.when(g + RELAY < groups)(lambda: kv_relay(g + RELAY))
+            pl.when(g + AHEAD < groups)(lambda: send_own(g + AHEAD))
+            qd_relay(g)
+        with jax.named_scope("kv_wait"):
+            kv_arrived(3, g)
+            kv_arrived(1, g)
+        with jax.named_scope("query"):
+            query_side(g)
+
+        @pl.when(g >= LAG)
         def _():
-            send_own(g + AHEAD)
-
-        kv_arrived(3, g)
-        kv_arrived(1, g)
-        query_side(g)
-
-        @pl.when(g > 0)
-        def _():
-            key_ready(g - 1)
-            key_side(g - 1)
+            with jax.named_scope("key_wait"):
+                key_ready(g - LAG)
+            with jax.named_scope("key"):
+                key_side(g - LAG)
 
         return carry
 
     lax.fori_loop(0, groups, step, 0)
 
     part = jnp.zeros((heads, T), F32)
-    for s in range(4):
-        part = part + dot_nt(pltpu.roll(dgb[s], 2 * T - 1, 1), onehot(0, s), precision=lax.Precision.HIGHEST)
+    with jax.named_scope("buckets"):
+        for s in range(4):
+            part = part + whole(dot_nt(thirds(pltpu.roll(dgb[s], 2 * T - 1, 1)), onehot(0, s)))
     xpart[...] = part
 
     def x_copy(t):
@@ -354,20 +414,31 @@
     for t in range(1, row):
         x_copy(t).start()
     xbuf[in_row] = xpart[pl.ds(pl.multiple_of(core * halves, halves), halves), :]
-    key_ready(groups - 1)
-    key_side(groups - 1)
-    for t in range(1, row):
-        x_copy(t).wait_recv()
-    ybuf[y_at] = total_of(xbuf, range(row))
+    with jax.named_scope("key"):
+        for g in range(groups - 4, groups - 2):
+            key_ready(g)
+            key_side(g)
+    with jax.named_scope("sum_x"):
+        for t in range(1, row):
+            x_copy(t).wait_recv()
+        ybuf[y_at] = total_of(xbuf, range(row))
     for t in range(1, ny):
         y_copy(t).start()
-    for t in range(1, ny):
-        y_copy(t).wait_recv()
-    zbuf[in_z] = total_of(ybuf, range(ny))
+    with jax.named_scope("key"):
+        key_ready(groups - 2)
+        key_side(groups - 2)
+    with jax.named_scope("sum_y"):
+        for t in range(1, ny):
+            y_copy(t).wait_recv()
+        zbuf[in_z] = total_of(ybuf, range(ny))
     for t in range(1, ring_z):
         z_copy(t).start()
-    for t in range(1, ring_z):
-        z_copy(t).wait_recv()
+    with jax.named_scope("key"):
+        key_ready(groups - 1)
+        key_side(groups - 1)
+    with jax.named_scope("sum_z"):
+        for t in range(1, ring_z):
+            z_copy(t).wait_recv()
     for h in range(n_head):
         for half in range(2):
             gb_ref[h * heads + half * halves : h * heads + (half + 1) * halves] = total_of(
@@ -376,22 +447,36 @@
 
     def drain(g, carry):
         for n in range(3):
-            kv_copy(n, g).wait_send()
-            qd_copy(n, g).wait_send()
+            pl.when(kv_sent[n])(lambda n=n: kv_copy(n, g).wait_send())
+            pl.when(qd_sent[n])(lambda n=n: qd_copy(n, g).wait_send())
         for s in (1, 2, 3):
-            st_copy(s, g).wait_send()
+            pl.when(me >= s)(lambda s=s: st_copy(s, g).wait_send())
         return carry
 
-    lax.fori_loop(0, groups, drain, 0)
+    with jax.named_scope("drain"):
+        lax.fori_loop(0, groups, drain, 0)
     for s in (1, 2, 3):
-        id_copy(s).wait_send()
-        mask_copy(s).wait_send()
+
+        @pl.when(me >= s)
+        def _():
+            id_copy(s).wait_send()
+            mask_copy(s).wait_send()
+
     for t in range(1, row):
         x_copy(t).wait_send()
     for t in range(1, ny):
         y_copy(t).wait_send()
     for t in range(1, ring_z):
         z_copy(t).wait_send()
+
+
+def put_out(*refs):
+    sems = refs[8]
+    copies = [pltpu.make_async_copy(refs[i], refs[4 + i], sems.at[i]) for i in range(4)]
+    for copy in copies:
+        copy.start()
+    for copy in copies:
+        copy.wait()
 
 
 def solution(mesh):
@@ -427,9 +512,10 @@
         in_hbm = pl.BlockSpec(memory_space=pltpu.HBM)
         in_vmem = pl.BlockSpec(memory_space=pltpu.VMEM)
         out = jax.ShapeDtypeStruct((tok, width), BF16)
-        return pl.pallas_call(
+        shapes = (out, out, out, jax.ShapeDtypeStruct((n_head * heads, buckets), F32))
+        results = pl.pallas_call(
             functools.partial(kernel, sizes),
-            out_shape=(out, out, out, jax.ShapeDtypeStruct((n_head * heads, buckets), F32)),
+            out_shape=shapes,
             in_specs=[in_hbm] * 7,
             out_specs=(in_vmem,) * 4,
             scratch_shapes=scratch,
@@ -437,6 +523,13 @@
                 collective_id=0, has_side_effects=True, vmem_limit_bytes=48 * 1024 * 1024
             ),
         )(*(pltpu.with_memory_space_constraint(x, pltpu.HBM) for x in operands))
+        return pl.pallas_call(
+            put_out,
+            out_shape=shapes,
+            in_specs=[in_vmem] * 4,
+            out_specs=(pl.BlockSpec(memory_space=pltpu.HBM),) * 4,
+            scratch_shapes=[dma((4,))],
+        )(*(pltpu.with_memory_space_constraint(x, pltpu.VMEM) for x in results))
 
     block = P("seq", "head")
     return jax.shard_map(

time: 91 us -> 49.1 us (0.54)
  Pallas kernels: 87.5 us -> 48.2 us
  local copies, waits for them, and re-layouts: 2.71 us -> 0 us
    pallas_call x1 -> x2, Pallas kernels: 87.5 us -> 48.2 us  [the longest x1 47.3 us: body(): pl.pallas_call(functools.partial(kernel, sizes), out_shape=shapes, in_spe...]
    unnamed x4 -> x0, local copies, waits for them, and re-layouts: 2.71 us -> none
where the time goes in v2:
time: 49.1 us; the launch traced here: 48.9 us
  Pallas kernels  48.2 us (98%)
  between operations  0.64 us (1%)
    pallas_call x1, Pallas kernels, body(): pl.pallas_call(functools.partial(kernel, sizes), out_shape=shapes, in_spe...  47.3 us

profile of v2, /device:TPU:1, one launch (start us, length us, event | category | flops | bytes accessed | tf_op | source)
XLA Modules:
  0.0 48.9 jit_solution(7045076940746170352)
XLA Ops:
  0.6 47.3 %shard_map.102 = (bf16[128,1024]{1,0:T(8,128)(2,1)S(1)}, bf16[128,1024]{1,0:T(8,128)(2,1)S(1)}, bf16[128,1024]{1,0:T(8,128)(2,1)S(1)}, f32[32,128]{1,0:T(8,128)S(1)}) custom-call(bf16[128,1024]{1,0:T(8,128)(2,1)} %q_hbm.1, bf16[128,1024]{1,0:T(8,128)(2,1)} %k_hbm.1, bf16[128,1024]{1,0:T(8,128)(2,1)} %v_hbm.1, bf16[128,1024]{1,0:T(8,128)(2,1)} %do_hbm.1, ...), custom_call_target="tpu_custom_call" | custom-call | tf_op jit(solution)/shard_map/pallas_call | solution.py:516
  48.0 0.9 %shard_map.103 = (bf16[128,1024]{1,0:T(8,128)(2,1)}, bf16[128,1024]{1,0:T(8,128)(2,1)}, bf16[128,1024]{1,0:T(8,128)(2,1)}, f32[32,128]{1,0:T(8,128)}) custom-call(bf16[128,1024]{1,0:T(8,128)(2,1)S(1)} %get-tuple-element.8.refs_0_, bf16[128,1024]{1,0:T(8,128)(2,1)S(1)} %get-tuple-element.9.refs_1_, bf16[128,1024]{1,0:T(8,128)(2,1)S(1)} %get-tuple-element.10.refs_2_, ...), custom_call_target="tpu_custom_call" | custom-call | tf_op jit(solution)/shard_map/pallas_call | solution.py:526

commit v3 on v2

--- a/solution.py
+++ b/solution.py
@@ -14,7 +14,7 @@
 BF16 = jnp.bfloat16
 AHEAD = 5
 RELAY = 2
-LAG = 4
+FIRST = 2
 NT = (((1,), (1,)), ((), ()))
 
 
@@ -33,12 +33,12 @@
     kv, qd, tableb, idsb, maskb, byb, biasq, biask,
     ss, sp, dsb, pb, ks, kp, kpb, kdsb, dk0b, dv0b, st, dgb,
     xpart, xbuf, ybuf, zbuf,
-    load_sem, small_sem, kv_send, kv_recv, qd_send, qd_recv,
-    st_send, st_recv, id_send, id_recv,
-    xs_sem, xr_sem, ys_sem, yr_sem, zs_sem, zr_sem,
+    load_sem, small_sem, kv_send, kv_recv, qd_send, qd_mid, qd_far,
+    st_send, st_recv, id_send, id_recv, sum_send, sum_recv,
 ):
     n_seq, nx, ny, nz, n_head, heads, groups = sizes
     T, W = 128, 128
+    half = groups // 2
     scale = 0.125
     c = scale * LOG2E
     me = lax.axis_index("seq")
@@ -72,12 +72,23 @@
         w_head = w // (2 * nz)
         return {"seq": w_z * (row * ny) + in_plane - core + w_core, "head": w_head}
 
+    barrier = pltpu.get_barrier_semaphore()
+    partners = [z_partner(t) for t in sorted(range(1, ring_z), key=lambda t: -min(t, ring_z - t))]
+    partners += [{"seq": y_partner(t)} for t in range(1, ny)]
+    partners += [{"seq": x_partner(t)} for t in range(1, row)]
+    partners += [{"seq": at(o)} for o in (1, 2, 3, -1, -2, -3)]
+    for other in partners:
+        pl.semaphore_signal(barrier, inc=1, device_id=other, device_id_type=MESH)
+
+    def all_of(ref, sem):
+        pltpu.make_async_copy(ref, ref, sem).wait()
+
     srcs = ((q_hbm, qd, 0), (do_hbm, qd, W), (k_hbm, kv, 0), (v_hbm, kv, W))
 
     def load(n, g):
         src, dst, off = srcs[n]
         return pltpu.make_async_copy(
-            src.at[:, pl.ds(g * W, W)], dst.at[g, pl.ds(0, T), pl.ds(off, W)], load_sem.at[n, g]
+            src.at[:, pl.ds(g * W, W)], dst.at[g, pl.ds(0, T), pl.ds(off, W)], load_sem.at[n]
         )
 
     for g in range(groups):
@@ -91,14 +102,6 @@
     for copy in small:
         copy.start()
 
-    barrier = pltpu.get_barrier_semaphore()
-    partners = [{"seq": at(o)} for o in (1, 2, 3, -1, -2, -3)]
-    partners += [{"seq": x_partner(t)} for t in range(1, row)]
-    partners += [{"seq": y_partner(t)} for t in range(1, ny)]
-    partners += [z_partner(t) for t in range(1, ring_z)]
-    for other in partners:
-        pl.semaphore_signal(barrier, inc=1, device_id=other, device_id_type=MESH)
-
     def remote(src, dst, send, recv, device):
         return pltpu.make_async_remote_copy(
             src_ref=src, dst_ref=dst, send_sem=send, recv_sem=recv, device_id=device, device_id_type=MESH
@@ -114,7 +117,7 @@
             src, s, device = slot(kv, g, 2), 3, at(1)
         else:
             src, s, device = slot(kv, g, pl.multiple_of(2 * core, 2)), 1, partner
-        return remote(src, slot(kv, g, s), kv_send.at[n, g], kv_recv.at[s - 1, g], {"seq": device})
+        return remote(src, slot(kv, g, s), kv_send.at[n], kv_recv.at[s - 1, g], {"seq": device})
 
     def qd_copy(n, g):
         if n == 0:
@@ -123,7 +126,8 @@
             src, s, device = slot(qd, g, 2), 3, at(-1)
         else:
             src, s, device = slot(qd, g, pl.multiple_of(2 - 2 * core, 2)), 1, partner
-        return remote(src, slot(qd, g, s), qd_send.at[n, g], qd_recv.at[s - 1, g], {"seq": device})
+        recv = qd_mid.at[g] if s == 2 else qd_far.at[s // 2, g // half]
+        return remote(src, slot(qd, g, s), qd_send.at[n], recv, {"seq": device})
 
     after = n_seq - 1 - me
     kv_sent = (after >= 2, jnp.logical_and(me >= 2, after >= 1), jnp.logical_or(core == 0, me >= 2))
@@ -139,11 +143,11 @@
     def kv_arrived(s, g):
         pl.when(me >= s)(lambda: kv_copy(by_slot[s], g).wait_recv())
 
-    def qd_arrived(s, g):
-        pl.when(after >= s)(lambda: qd_copy(by_slot[s], g).wait_recv())
+    def qd_arrived(g):
+        pl.when(after >= 2)(lambda: qd_copy(0, g).wait_recv())
 
     def st_copy(s, g):
-        return remote(st.at[0, g], st.at[s, g], st_send.at[s - 1, g], st_recv.at[s - 1, g], {"seq": at(-s)})
+        return remote(st.at[0, g], st.at[s, g], st_send.at[s - 1], st_recv.at[s - 1, g // half], {"seq": at(-s)})
 
     def id_copy(s):
         return remote(idsb.at[0], idsb.at[s], id_send.at[0, s - 1], id_recv.at[0, s - 1], {"seq": at(-s)})
@@ -161,16 +165,16 @@
         kv_start(2, g)
 
     def qd_relay(g):
-        qd_arrived(2, g)
+        qd_arrived(g)
         qd_start(1, g)
         qd_start(2, g)
 
     with jax.named_scope("load_wait"):
         for copy in small:
             copy.wait()
-        for g in range(groups):
-            for n in (2, 3, 0, 1):
-                load(n, g).wait()
+        for n in (2, 3, 0, 1):
+            src, dst, off = srcs[n]
+            all_of(dst.at[:, pl.ds(0, T), pl.ds(off, W)], load_sem.at[n])
     with jax.named_scope("barrier"):
         pl.semaphore_wait(barrier, len(partners))
     for s in (1, 2, 3):
@@ -180,7 +184,7 @@
             id_copy(s).start()
             mask_copy(s).start()
 
-    for g in range(AHEAD):
+    for g in range(FIRST):
         send_own(g)
     for s in (1, 2, 3):
 
@@ -248,16 +252,11 @@
     with jax.named_scope("build_query"):
         lax.fori_loop(0, groups, build_query, 0)
     with jax.named_scope("relay_first"):
-        kv_relay(0)
-    with jax.named_scope("by_key"):
-        for s in (1, 2, 3):
-
-            @pl.when(after >= s)
-            def _():
-                id_copy(s).wait_recv()
-                mask_copy(s).wait_recv()
-
-            byb[3 + s] = by_offset(s, s, after >= s)
+        for g in range(RELAY):
+            kv_relay(g)
+            send_own(FIRST + g)
+    for g in range(FIRST + RELAY, AHEAD):
+        send_own(g)
 
     def build_key(g, carry):
         for h in range(2):
@@ -267,11 +266,16 @@
                     biask[g, pl.ds(h * T + 8 * a, 8), pl.ds((s - 1) * T, T)] = block_row(low, high, a)
         return carry
 
-    with jax.named_scope("build_key"):
+    def build_keys():
+        for s in (1, 2, 3):
+
+            @pl.when(after >= s)
+            def _():
+                id_copy(s).wait_recv()
+                mask_copy(s).wait_recv()
+
+            byb[3 + s] = by_offset(s, s, after >= s)
         lax.fori_loop(0, groups, build_key, 0)
-    with jax.named_scope("relay_first"):
-        for g in range(1, RELAY):
-            kv_relay(g)
 
     def two(x):
         zero = jnp.zeros_like(x)
@@ -363,11 +367,19 @@
         dv_ref[:, pl.ds(g * W, W)] = (merged(dot_nn(kpb[...], dos)) + dv0b[g]).astype(BF16)
         dk_ref[:, pl.ds(g * W, W)] = ((merged(dot_nn(kdsb[...], qs)) + dk0b[g]) * scale).astype(BF16)
 
-    def key_ready(g):
+    def key_ready(part):
+        chunks = pl.ds(part * half, half)
         for s in (1, 3):
-            qd_arrived(s, g)
+            pl.when(after >= s)(lambda s=s: all_of(qd.at[chunks, pl.ds(s * T, T)], qd_far.at[s // 2, part]))
         for s in (1, 2, 3):
-            pl.when(after >= s)(lambda s=s: st_copy(s, g).wait_recv())
+            pl.when(after >= s)(lambda s=s: all_of(st.at[s, chunks], st_recv.at[s - 1, part]))
+
+    def keys(start, stop):
+        def one(g, carry):
+            key_side(g)
+            return carry
+
+        lax.fori_loop(start, stop, one, 0)
 
     def step(g, carry):
         with jax.named_scope("relay"):
@@ -379,14 +391,6 @@
             kv_arrived(1, g)
         with jax.named_scope("query"):
             query_side(g)
-
-        @pl.when(g >= LAG)
-        def _():
-            with jax.named_scope("key_wait"):
-                key_ready(g - LAG)
-            with jax.named_scope("key"):
-                key_side(g - LAG)
-
         return carry
 
     lax.fori_loop(0, groups, step, 0)
@@ -399,14 +403,14 @@
 
     def x_copy(t):
         other = x_partner(t)
-        half = pl.multiple_of(lax.rem(other, 2) * halves, halves)
-        return remote(xpart.at[pl.ds(half, halves)], xbuf.at[in_row], xs_sem.at[t - 1], xr_sem.at[t - 1], {"seq": other})
+        start = pl.multiple_of(lax.rem(other, 2) * halves, halves)
+        return remote(xpart.at[pl.ds(start, halves)], xbuf.at[in_row], sum_send.at[0], sum_recv.at[0], {"seq": other})
 
     def y_copy(t):
-        return remote(ybuf.at[y_at], ybuf.at[y_at], ys_sem.at[t - 1], yr_sem.at[t - 1], {"seq": y_partner(t)})
+        return remote(ybuf.at[y_at], ybuf.at[y_at], sum_send.at[1], sum_recv.at[1], {"seq": y_partner(t)})
 
     def z_copy(t):
-        return remote(zbuf.at[in_z], zbuf.at[in_z], zs_sem.at[t - 1], zr_sem.at[t - 1], z_partner(t))
+        return remote(zbuf.at[in_z], zbuf.at[in_z], sum_send.at[2], sum_recv.at[2], z_partner(t))
 
     def total_of(buf, slots):
         return functools.reduce(jnp.add, [buf[i] for i in slots])
@@ -414,60 +418,51 @@
     for t in range(1, row):
         x_copy(t).start()
     xbuf[in_row] = xpart[pl.ds(pl.multiple_of(core * halves, halves), halves), :]
-    with jax.named_scope("key"):
-        for g in range(groups - 4, groups - 2):
-            key_ready(g)
-            key_side(g)
+    with jax.named_scope("build_key"):
+        build_keys()
     with jax.named_scope("sum_x"):
-        for t in range(1, row):
-            x_copy(t).wait_recv()
+        all_of(xbuf.at[pl.ds(0, row - 1)], sum_recv.at[0])
         ybuf[y_at] = total_of(xbuf, range(row))
     for t in range(1, ny):
         y_copy(t).start()
+    with jax.named_scope("key_wait"):
+        key_ready(0)
     with jax.named_scope("key"):
-        key_ready(groups - 2)
-        key_side(groups - 2)
+        keys(0, half - 1)
     with jax.named_scope("sum_y"):
-        for t in range(1, ny):
-            y_copy(t).wait_recv()
+        if ny > 1:
+            all_of(ybuf.at[pl.ds(0, ny - 1)], sum_recv.at[1])
         zbuf[in_z] = total_of(ybuf, range(ny))
     for t in range(1, ring_z):
         z_copy(t).start()
+    with jax.named_scope("key_wait"):
+        key_ready(1)
     with jax.named_scope("key"):
-        key_ready(groups - 1)
-        key_side(groups - 1)
+        keys(half - 1, groups)
     with jax.named_scope("sum_z"):
-        for t in range(1, ring_z):
-            z_copy(t).wait_recv()
+        all_of(zbuf.at[pl.ds(0, ring_z - 1)], sum_recv.at[2])
     for h in range(n_head):
-        for half in range(2):
-            gb_ref[h * heads + half * halves : h * heads + (half + 1) * halves] = total_of(
-                zbuf, [(h * nz + z) * 2 + half for z in range(nz)]
+        for side in range(2):
+            gb_ref[h * heads + side * halves : h * heads + (side + 1) * halves] = total_of(
+                zbuf, [(h * nz + z) * 2 + side for z in range(nz)]
             )
 
-    def drain(g, carry):
+    with jax.named_scope("drain"):
         for n in range(3):
-            pl.when(kv_sent[n])(lambda n=n: kv_copy(n, g).wait_send())
-            pl.when(qd_sent[n])(lambda n=n: qd_copy(n, g).wait_send())
+            pl.when(kv_sent[n])(lambda n=n: all_of(kv.at[:, pl.ds(0, T)], kv_send.at[n]))
+            pl.when(qd_sent[n])(lambda n=n: all_of(qd.at[:, pl.ds(0, T)], qd_send.at[n]))
         for s in (1, 2, 3):
-            pl.when(me >= s)(lambda s=s: st_copy(s, g).wait_send())
-        return carry
-
-    with jax.named_scope("drain"):
-        lax.fori_loop(0, groups, drain, 0)
-    for s in (1, 2, 3):
-
-        @pl.when(me >= s)
-        def _():
-            id_copy(s).wait_send()
-            mask_copy(s).wait_send()
-
-    for t in range(1, row):
-        x_copy(t).wait_send()
-    for t in range(1, ny):
-        y_copy(t).wait_send()
-    for t in range(1, ring_z):
-        z_copy(t).wait_send()
+
+            @pl.when(me >= s)
+            def _():
+                all_of(st.at[0], st_send.at[s - 1])
+                id_copy(s).wait_send()
+                mask_copy(s).wait_send()
+
+        all_of(xbuf.at[pl.ds(0, row - 1)], sum_send.at[0])
+        if ny > 1:
+            all_of(ybuf.at[pl.ds(0, ny - 1)], sum_send.at[1])
+        all_of(zbuf.at[pl.ds(0, ring_z - 1)], sum_send.at[2])
 
 
 def put_out(*refs):
@@ -503,11 +498,8 @@
             V((4, groups, 8, 128), F32), V((4, heads, 256), F32),
             V((heads, 128), F32), V((row, heads // 2, 128), F32), V((ny, heads // 2, 128), F32),
             V((ring_z, heads // 2, 128), F32),
-            dma((4, groups)), dma((3,)),
-            dma((3, groups)), dma((3, groups)), dma((3, groups)), dma((3, groups)),
-            dma((3, groups)), dma((3, groups)), dma((2, 3)), dma((2, 3)),
-            dma((row - 1,)), dma((row - 1,)), dma((max(ny - 1, 1),)), dma((max(ny - 1, 1),)),
-            dma((ring_z - 1,)), dma((ring_z - 1,)),
+            dma((4,)), dma((3,)), dma((3,)), dma((3, groups)), dma((3,)), dma((groups,)), dma((2, 2)),
+            dma((3,)), dma((3, 2)), dma((2, 3)), dma((2, 3)), dma((3,)), dma((3,)),
         ]
         in_hbm = pl.BlockSpec(memory_space=pltpu.HBM)
         in_vmem = pl.BlockSpec(memory_space=pltpu.VMEM)

time: 49.1 us -> 47 us (0.957)
  Pallas kernels: 48.2 us -> 46.1 us
    pallas_call x1, Pallas kernels: 47.3 us -> 45.2 us  [body(): pl.pallas_call(functools.partial(kernel, sizes), out_shape=shapes, in_spe...]
where the time goes in v3:
time: 47 us; the launch traced here: 46.8 us
  Pallas kernels  46.1 us (98%)
  between operations  0.64 us (1%)
    pallas_call x1, Pallas kernels, body(): pl.pallas_call(functools.partial(kernel, sizes), out_shape=shapes, in_spe...  45.2 us

profile of v3, /device:TPU:1, one launch (start us, length us, event | category | flops | bytes accessed | tf_op | source)
XLA Modules:
  0.0 46.8 jit_solution(314828897334930684)
XLA Ops:
  0.6 45.2 %shard_map.102 = (bf16[128,1024]{1,0:T(8,128)(2,1)S(1)}, bf16[128,1024]{1,0:T(8,128)(2,1)S(1)}, bf16[128,1024]{1,0:T(8,128)(2,1)S(1)}, f32[32,128]{1,0:T(8,128)S(1)}) custom-call(bf16[128,1024]{1,0:T(8,128)(2,1)} %q_hbm.1, bf16[128,1024]{1,0:T(8,128)(2,1)} %k_hbm.1, bf16[128,1024]{1,0:T(8,128)(2,1)} %v_hbm.1, bf16[128,1024]{1,0:T(8,128)(2,1)} %do_hbm.1, ...), custom_call_target="tpu_custom_call" | custom-call | tf_op jit(solution)/shard_map/pallas_call | solution.py:508
  45.9 0.9 %shard_map.103 = (bf16[128,1024]{1,0:T(8,128)(2,1)}, bf16[128,1024]{1,0:T(8,128)(2,1)}, bf16[128,1024]{1,0:T(8,128)(2,1)}, f32[32,128]{1,0:T(8,128)}) custom-call(bf16[128,1024]{1,0:T(8,128)(2,1)S(1)} %get-tuple-element.8.refs_0_, bf16[128,1024]{1,0:T(8,128)(2,1)S(1)} %get-tuple-element.9.refs_1_, bf16[128,1024]{1,0:T(8,128)(2,1)S(1)} %get-tuple-element.10.refs_2_, ...), custom_call_target="tpu_custom_call" | custom-call | tf_op jit(solution)/shard_map/pallas_call | solution.py:518

commit v4 on v3

--- a/solution.py
+++ b/solution.py
@@ -72,28 +72,23 @@
         w_head = w // (2 * nz)
         return {"seq": w_z * (row * ny) + in_plane - core + w_core, "head": w_head}
 
-    barrier = pltpu.get_barrier_semaphore()
-    partners = [z_partner(t) for t in sorted(range(1, ring_z), key=lambda t: -min(t, ring_z - t))]
-    partners += [{"seq": y_partner(t)} for t in range(1, ny)]
-    partners += [{"seq": x_partner(t)} for t in range(1, row)]
-    partners += [{"seq": at(o)} for o in (1, 2, 3, -1, -2, -3)]
-    for other in partners:
-        pl.semaphore_signal(barrier, inc=1, device_id=other, device_id_type=MESH)
-
     def all_of(ref, sem):
         pltpu.make_async_copy(ref, ref, sem).wait()
 
-    srcs = ((q_hbm, qd, 0), (do_hbm, qd, W), (k_hbm, kv, 0), (v_hbm, kv, W))
-
-    def load(n, g):
-        src, dst, off = srcs[n]
-        return pltpu.make_async_copy(
-            src.at[:, pl.ds(g * W, W)], dst.at[g, pl.ds(0, T), pl.ds(off, W)], load_sem.at[n]
-        )
-
-    for g in range(groups):
-        for n in (2, 3, 0, 1):
-            load(n, g).start()
+    srcs = ((k_hbm, kv, 0, 0), (v_hbm, kv, W, 0), (q_hbm, qd, 0, 1), (do_hbm, qd, W, 1))
+
+    def load(chunks, part):
+        for g in chunks:
+            for src, dst, off, n in srcs:
+                pltpu.make_async_copy(
+                    src.at[:, pl.ds(g * W, W)], dst.at[g, pl.ds(0, T), pl.ds(off, W)], load_sem.at[part, n]
+                ).start()
+
+    def loaded(start, count, part):
+        for n, buf in enumerate((kv, qd)):
+            all_of(buf.at[pl.ds(start, count), pl.ds(0, T)], load_sem.at[part, n])
+
+    load(range(FIRST), 0)
     small = [
         pltpu.make_async_copy(table_hbm, tableb, small_sem.at[0]),
         pltpu.make_async_copy(ids_hbm.at[0], idsb.at[0], small_sem.at[1]),
@@ -101,6 +96,18 @@
     ]
     for copy in small:
         copy.start()
+
+    def far_first(count):
+        return sorted(range(1, count), key=lambda t: -min(t, count - t))
+
+    barrier = pltpu.get_barrier_semaphore()
+    partners = [z_partner(t) for t in far_first(ring_z)]
+    partners += [{"seq": y_partner(t)} for t in far_first(ny)]
+    partners += [{"seq": x_partner(t)} for t in far_first(row)]
+    partners += [{"seq": at(o)} for o in (3, -3, 2, -2, 1, -1)]
+    for other in partners:
+        pl.semaphore_signal(barrier, inc=1, device_id=other, device_id_type=MESH)
+    load(range(FIRST, groups), 1)
 
     def remote(src, dst, send, recv, device):
         return pltpu.make_async_remote_copy(
@@ -170,11 +177,9 @@
         qd_start(2, g)
 
     with jax.named_scope("load_wait"):
+        loaded(0, FIRST, 0)
         for copy in small:
             copy.wait()
-        for n in (2, 3, 0, 1):
-            src, dst, off = srcs[n]
-            all_of(dst.at[:, pl.ds(0, T), pl.ds(off, W)], load_sem.at[n])
     with jax.named_scope("barrier"):
         pl.semaphore_wait(barrier, len(partners))
     for s in (1, 2, 3):
@@ -186,6 +191,7 @@
 
     for g in range(FIRST):
         send_own(g)
+    loaded(FIRST, groups - FIRST, 1)
     for s in (1, 2, 3):
 
         @pl.when(me < s)
@@ -251,12 +257,11 @@
 
     with jax.named_scope("build_query"):
         lax.fori_loop(0, groups, build_query, 0)
+    send_own(FIRST)
     with jax.named_scope("relay_first"):
         for g in range(RELAY):
             kv_relay(g)
-            send_own(FIRST + g)
-    for g in range(FIRST + RELAY, AHEAD):
-        send_own(g)
+            send_own(FIRST + 1 + g)
 
     def build_key(g, carry):
         for h in range(2):
@@ -266,7 +271,7 @@
                     biask[g, pl.ds(h * T + 8 * a, 8), pl.ds((s - 1) * T, T)] = block_row(low, high, a)
         return carry
 
-    def build_keys():
+    with jax.named_scope("by_key"):
         for s in (1, 2, 3):
 
             @pl.when(after >= s)
@@ -275,7 +280,6 @@
                 mask_copy(s).wait_recv()
 
             byb[3 + s] = by_offset(s, s, after >= s)
-        lax.fori_loop(0, groups, build_key, 0)
 
     def two(x):
         zero = jnp.zeros_like(x)
@@ -290,7 +294,7 @@
         parts = [x[8 * j : 8 * j + 8] for j in range(x.shape[0] // 8)]
         return functools.reduce(op, parts)
 
-    def query_side(g):
+    def query_scores(g):
         q2, do2 = qd[g, 0:T, 0:W], qd[g, 0:T, W : 2 * W]
         ss[...] = dot_nt(kv[g, :, 0:W], two(q2))
         sp[...] = dot_nt(kv[g, :, W : 2 * W], two(do2))
@@ -341,6 +345,9 @@
                 for by in (1, 2, 4):
                     both = both + pltpu.roll(pltpu.roll(both, 2 * T - by, 1), 8 - by, 0)
                 dgb[s, pl.ds(2 * g + h, 1), :] = both[0:1]
+
+    def query_grads(g):
+        q2, do2 = qd[g, 0:T, 0:W], qd[g, 0:T, W : 2 * W]
         turned = dot_nn(kv[g, :, 0:W].T, dsb[...])
         joined = jnp.concatenate([turned[0:64, 0:T], turned[64:T, T : 2 * T]], axis=0)
         dq_ref[:, pl.ds(g * W, W)] = (joined.T * scale).astype(BF16)
@@ -390,10 +397,17 @@
             kv_arrived(3, g)
             kv_arrived(1, g)
         with jax.named_scope("query"):
-            query_side(g)
+            query_scores(g)
+            query_grads(g)
         return carry
 
-    lax.fori_loop(0, groups, step, 0)
+    lax.fori_loop(0, groups - 1, step, 0)
+    qd_relay(groups - 1)
+    with jax.named_scope("kv_wait"):
+        kv_arrived(3, groups - 1)
+        kv_arrived(1, groups - 1)
+    with jax.named_scope("query"):
+        query_scores(groups - 1)
 
     part = jnp.zeros((heads, T), F32)
     with jax.named_scope("buckets"):
@@ -415,30 +429,32 @@
     def total_of(buf, slots):
         return functools.reduce(jnp.add, [buf[i] for i in slots])
 
-    for t in range(1, row):
+    for t in far_first(row):
         x_copy(t).start()
     xbuf[in_row] = xpart[pl.ds(pl.multiple_of(core * halves, halves), halves), :]
+    with jax.named_scope("grads"):
+        query_grads(groups - 1)
     with jax.named_scope("build_key"):
-        build_keys()
+        lax.fori_loop(0, groups, build_key, 0)
     with jax.named_scope("sum_x"):
         all_of(xbuf.at[pl.ds(0, row - 1)], sum_recv.at[0])
         ybuf[y_at] = total_of(xbuf, range(row))
-    for t in range(1, ny):
+    for t in far_first(ny):
         y_copy(t).start()
     with jax.named_scope("key_wait"):
         key_ready(0)
     with jax.named_scope("key"):
-        keys(0, half - 1)
+        keys(0, 2)
     with jax.named_scope("sum_y"):
         if ny > 1:
             all_of(ybuf.at[pl.ds(0, ny - 1)], sum_recv.at[1])
         zbuf[in_z] = total_of(ybuf, range(ny))
-    for t in range(1, ring_z):
+    for t in far_first(ring_z):
         z_copy(t).start()
     with jax.named_scope("key_wait"):
         key_ready(1)
     with jax.named_scope("key"):
-        keys(half - 1, groups)
+        keys(2, groups)
     with jax.named_scope("sum_z"):
         all_of(zbuf.at[pl.ds(0, ring_z - 1)], sum_recv.at[2])
     for h in range(n_head):
@@ -498,7 +514,7 @@
             V((4, groups, 8, 128), F32), V((4, heads, 256), F32),
             V((heads, 128), F32), V((row, heads // 2, 128), F32), V((ny, heads // 2, 128), F32),
             V((ring_z, heads // 2, 128), F32),
-            dma((4,)), dma((3,)), dma((3,)), dma((3, groups)), dma((3,)), dma((groups,)), dma((2, 2)),
+            dma((2, 2)), dma((3,)), dma((3,)), dma((3, groups)), dma((3,)), dma((groups,)), dma((2, 2)),
             dma((3,)), dma((3, 2)), dma((2, 3)), dma((2, 3)), dma((3,)), dma((3,)),
         ]
         in_hbm = pl.BlockSpec(memory_space=pltpu.HBM)

time: 47 us -> 45.4 us (0.966)
  Pallas kernels: 46.1 us -> 44.6 us
    pallas_call x1, Pallas kernels: 45.2 us -> 43.6 us  [body(): pl.pallas_call(functools.partial(kernel, sizes), out_shape=shapes, in_spe...]
where the time goes in v4:
time: 45.4 us; the launch traced here: 45.2 us
  Pallas kernels  44.6 us (98%)
  between operations  0.64 us (1%)
    pallas_call x1, Pallas kernels, body(): pl.pallas_call(functools.partial(kernel, sizes), out_shape=shapes, in_spe...  43.6 us
    pallas_call x1, Pallas kernels, body(): pl.pallas_call(put_out, out_shape=shapes, in_specs=[in_vmem] * 4, out_spe...  0.91 us

profile of v4, /device:TPU:1, one launch (start us, length us, event | category | flops | bytes accessed | tf_op | source)
XLA Modules:
  0.0 45.2 jit_solution(12949059127044237968)
XLA Ops:
  0.6 43.6 %shard_map.102 = (bf16[128,1024]{1,0:T(8,128)(2,1)S(1)}, bf16[128,1024]{1,0:T(8,128)(2,1)S(1)}, bf16[128,1024]{1,0:T(8,128)(2,1)S(1)}, f32[32,128]{1,0:T(8,128)S(1)}) custom-call(bf16[128,1024]{1,0:T(8,128)(2,1)} %q_hbm.1, bf16[128,1024]{1,0:T(8,128)(2,1)} %k_hbm.1, bf16[128,1024]{1,0:T(8,128)(2,1)} %v_hbm.1, bf16[128,1024]{1,0:T(8,128)(2,1)} %do_hbm.1, ...), custom_call_target="tpu_custom_call" | custom-call | tf_op jit(solution)/shard_map/pallas_call | solution.py:524
  44.3 0.9 %shard_map.103 = (bf16[128,1024]{1,0:T(8,128)(2,1)}, bf16[128,1024]{1,0:T(8,128)(2,1)}, bf16[128,1024]{1,0:T(8,128)(2,1)}, f32[32,128]{1,0:T(8,128)}) custom-call(bf16[128,1024]{1,0:T(8,128)(2,1)S(1)} %get-tuple-element.8.refs_0_, bf16[128,1024]{1,0:T(8,128)(2,1)S(1)} %get-tuple-element.9.refs_1_, bf16[128,1024]{1,0:T(8,128)(2,1)S(1)} %get-tuple-element.10.refs_2_, ...), custom_call_target="tpu_custom_call" | custom-call | tf_op jit(solution)/shard_map/pallas_call | solution.py:534

commit v5 on v4

--- a/solution.py
+++ b/solution.py
@@ -14,7 +14,9 @@
 BF16 = jnp.bfloat16
 AHEAD = 5
 RELAY = 2
-FIRST = 2
+FIRST = 3
+DEFER = 4
+LAST_KEY = 7
 NT = (((1,), (1,)), ((), ()))
 
 
@@ -32,7 +34,7 @@
     dq_ref, dk_ref, dv_ref, gb_ref,
     kv, qd, tableb, idsb, maskb, byb, biasq, biask,
     ss, sp, dsb, pb, ks, kp, kpb, kdsb, dk0b, dv0b, st, dgb,
-    xpart, xbuf, ybuf, zbuf,
+    xpart, xpair, xbuf, ybuf, zbuf, gbuf,
     load_sem, small_sem, kv_send, kv_recv, qd_send, qd_mid, qd_far,
     st_send, st_recv, id_send, id_recv, sum_send, sum_recv,
 ):
@@ -50,27 +52,34 @@
         return lax.rem(me + (offset + n_seq), n_seq)
 
     row = 2 * nx
-    in_row = lax.rem(me, row)
-    row_base = me - in_row
+    x_at = lax.rem(me, row) // 2
     y_at = lax.rem(me // row, ny)
     z_at = me // (row * ny)
-    in_plane = lax.rem(me, row * ny)
-    halves = heads // 2
-    ring_z = n_head * nz * 2
-    in_z = (hi * nz + z_at) * 2 + core
+    ring_z = n_head * nz
+    in_z = hi * nz + z_at
 
     def x_partner(t):
-        return row_base + lax.rem(in_row + t, row)
+        return {"seq": me + 2 * (lax.rem(x_at + t, nx) - x_at)}
 
     def y_partner(t):
-        return z_at * (row * ny) + lax.rem(y_at + t, ny) * row + in_row
+        return {"seq": me + row * (lax.rem(y_at + t, ny) - y_at)}
 
     def z_partner(t):
         w = lax.rem(in_z + t, ring_z)
-        w_core = lax.rem(w, 2)
-        w_z = lax.rem(w // 2, nz)
-        w_head = w // (2 * nz)
-        return {"seq": w_z * (row * ny) + in_plane - core + w_core, "head": w_head}
+        return {"seq": me + row * ny * (lax.rem(w, nz) - z_at), "head": w // nz}
+
+    def far_first(count):
+        return sorted(range(1, count), key=lambda t: -min(t, count - t))
+
+    barrier = pltpu.get_barrier_semaphore()
+
+    def signal(other):
+        pl.semaphore_signal(barrier, inc=1, device_id=other, device_id_type=MESH)
+
+    @pl.when(core == 1)
+    def _():
+        for t in far_first(ring_z):
+            signal(z_partner(t))
 
     def all_of(ref, sem):
         pltpu.make_async_copy(ref, ref, sem).wait()
@@ -97,16 +106,17 @@
     for copy in small:
         copy.start()
 
-    def far_first(count):
-        return sorted(range(1, count), key=lambda t: -min(t, count - t))
-
-    barrier = pltpu.get_barrier_semaphore()
-    partners = [z_partner(t) for t in far_first(ring_z)]
-    partners += [{"seq": y_partner(t)} for t in far_first(ny)]
-    partners += [{"seq": x_partner(t)} for t in far_first(row)]
-    partners += [{"seq": at(o)} for o in (3, -3, 2, -2, 1, -1)]
-    for other in partners:
-        pl.semaphore_signal(barrier, inc=1, device_id=other, device_id_type=MESH)
+    @pl.when(core == 1)
+    def _():
+        for t in far_first(ny):
+            signal(y_partner(t))
+        for t in far_first(nx):
+            signal(x_partner(t))
+
+    near = jnp.minimum(me, 3) + jnp.minimum(n_seq - 1 - me, 3)
+    for o in (3, 2, 1):
+        pl.when(me >= o)(lambda o=o: signal({"seq": me - o}))
+        pl.when(me + o < n_seq)(lambda o=o: signal({"seq": me + o}))
     load(range(FIRST, groups), 1)
 
     def remote(src, dst, send, recv, device):
@@ -181,7 +191,7 @@
         for copy in small:
             copy.wait()
     with jax.named_scope("barrier"):
-        pl.semaphore_wait(barrier, len(partners))
+        pl.semaphore_wait(barrier, near + core * (ring_z + ny + nx - 3))
     for s in (1, 2, 3):
 
         @pl.when(me >= s)
@@ -261,7 +271,8 @@
     with jax.named_scope("relay_first"):
         for g in range(RELAY):
             kv_relay(g)
-            send_own(FIRST + 1 + g)
+            if FIRST + 1 + g < AHEAD:
+                send_own(FIRST + 1 + g)
 
     def build_key(g, carry):
         for h in range(2):
@@ -326,9 +337,9 @@
             for r in range(s * T, s * T + T, R):
                 p = ss[r : r + R] * inverse
                 ds = p * (sp[r : r + R] - delta)
-                dsb[r : r + R] = ds.astype(BF16)
+                dsb[g, r : r + R] = ds.astype(BF16)
                 if s == 0:
-                    pb[r : r + R] = p.astype(BF16)
+                    pb[g, r : r + R] = p.astype(BF16)
                 for j in range(R // 8):
                     a = (r - s * T) // 8 + j
                     for h in range(2):
@@ -346,15 +357,17 @@
                     both = both + pltpu.roll(pltpu.roll(both, 2 * T - by, 1), 8 - by, 0)
                 dgb[s, pl.ds(2 * g + h, 1), :] = both[0:1]
 
+    def st_start(g):
+        for s in (1, 2, 3):
+            pl.when(me >= s)(lambda s=s: st_copy(s, g).start())
+
     def query_grads(g):
         q2, do2 = qd[g, 0:T, 0:W], qd[g, 0:T, W : 2 * W]
-        turned = dot_nn(kv[g, :, 0:W].T, dsb[...])
+        turned = dot_nn(kv[g, :, 0:W].T, dsb[g])
         joined = jnp.concatenate([turned[0:64, 0:T], turned[64:T, T : 2 * T]], axis=0)
         dq_ref[:, pl.ds(g * W, W)] = (joined.T * scale).astype(BF16)
-        for s in (1, 2, 3):
-            pl.when(me >= s)(lambda s=s: st_copy(s, g).start())
-        dv0b[g] = jnp.where(first, dot_nn(pb[:, 0:T], do2), dot_nn(pb[:, T : 2 * T], do2))
-        dk0b[g] = jnp.where(first, dot_nn(dsb[0:T, 0:T], q2), dot_nn(dsb[0:T, T : 2 * T], q2))
+        dv0b[g] = jnp.where(first, dot_nn(pb[g, :, 0:T], do2), dot_nn(pb[g, :, T : 2 * T], do2))
+        dk0b[g] = jnp.where(first, dot_nn(dsb[g, 0:T, 0:T], q2), dot_nn(dsb[g, 0:T, T : 2 * T], q2))
 
     def key_side(g):
         qs, dos = qd[g, T : 4 * T, 0:W], qd[g, T : 4 * T, W : 2 * W]
@@ -398,7 +411,13 @@
             kv_arrived(1, g)
         with jax.named_scope("query"):
             query_scores(g)
-            query_grads(g)
+            st_start(g)
+
+        @pl.when(g < groups - DEFER)
+        def _():
+            with jax.named_scope("grads"):
+                query_grads(g)
+
         return carry
 
     lax.fori_loop(0, groups - 1, step, 0)
@@ -415,13 +434,17 @@
             part = part + whole(dot_nt(thirds(pltpu.roll(dgb[s], 2 * T - 1, 1)), onehot(0, s)))
     xpart[...] = part
 
+    def pair_copy():
+        return remote(xpart, xpair, sum_send.at[3], sum_recv.at[3], {"seq": partner})
+
+    def result_copy():
+        return remote(gbuf, gbuf, sum_send.at[4], sum_recv.at[4], {"seq": partner})
+
     def x_copy(t):
-        other = x_partner(t)
-        start = pl.multiple_of(lax.rem(other, 2) * halves, halves)
-        return remote(xpart.at[pl.ds(start, halves)], xbuf.at[in_row], sum_send.at[0], sum_recv.at[0], {"seq": other})
+        return remote(xbuf.at[x_at], xbuf.at[x_at], sum_send.at[0], sum_recv.at[0], x_partner(t))
 
     def y_copy(t):
-        return remote(ybuf.at[y_at], ybuf.at[y_at], sum_send.at[1], sum_recv.at[1], {"seq": y_partner(t)})
+        return remote(ybuf.at[y_at], ybuf.at[y_at], sum_send.at[1], sum_recv.at[1], y_partner(t))
 
     def z_copy(t):
         return remote(zbuf.at[in_z], zbuf.at[in_z], sum_send.at[2], sum_recv.at[2], z_partner(t))
@@ -429,39 +452,73 @@
     def total_of(buf, slots):
         return functools.reduce(jnp.add, [buf[i] for i in slots])
 
-    for t in far_first(row):
-        x_copy(t).start()
-    xbuf[in_row] = xpart[pl.ds(pl.multiple_of(core * halves, halves), halves), :]
+    @pl.when(core == 0)
+    def _():
+        pair_copy().start()
+
+    @pl.when(core == 1)
+    def _():
+        with jax.named_scope("sum_pair"):
+            pair_copy().wait_recv()
+            xbuf[x_at] = xpair[...] + xpart[...]
+        for t in far_first(nx):
+            x_copy(t).start()
+
     with jax.named_scope("grads"):
-        query_grads(groups - 1)
+        st_start(groups - 1)
+
+        def late(g, carry):
+            query_grads(g)
+            return carry
+
+        lax.fori_loop(groups - DEFER, groups, late, 0)
+
+    @pl.when(core == 1)
+    def _():
+        with jax.named_scope("sum_x"):
+            all_of(xbuf.at[pl.ds(0, nx - 1)], sum_recv.at[0])
+            ybuf[y_at] = total_of(xbuf, range(nx))
+        for t in far_first(ny):
+            y_copy(t).start()
+
     with jax.named_scope("build_key"):
         lax.fori_loop(0, groups, build_key, 0)
-    with jax.named_scope("sum_x"):
-        all_of(xbuf.at[pl.ds(0, row - 1)], sum_recv.at[0])
-        ybuf[y_at] = total_of(xbuf, range(row))
-    for t in far_first(ny):
-        y_copy(t).start()
+
+    @pl.when(core == 1)
+    def _():
+        with jax.named_scope("sum_y"):
+            if ny > 1:
+                all_of(ybuf.at[pl.ds(0, ny - 1)], sum_recv.at[1])
+            zbuf[in_z] = total_of(ybuf, range(ny))
+        for t in far_first(ring_z):
+            z_copy(t).start()
+
     with jax.named_scope("key_wait"):
         key_ready(0)
     with jax.named_scope("key"):
         keys(0, 2)
-    with jax.named_scope("sum_y"):
-        if ny > 1:
-            all_of(ybuf.at[pl.ds(0, ny - 1)], sum_recv.at[1])
-        zbuf[in_z] = total_of(ybuf, range(ny))
-    for t in far_first(ring_z):
-        z_copy(t).start()
     with jax.named_scope("key_wait"):
         key_ready(1)
     with jax.named_scope("key"):
-        keys(2, groups)
-    with jax.named_scope("sum_z"):
-        all_of(zbuf.at[pl.ds(0, ring_z - 1)], sum_recv.at[2])
-    for h in range(n_head):
-        for side in range(2):
-            gb_ref[h * heads + side * halves : h * heads + (side + 1) * halves] = total_of(
-                zbuf, [(h * nz + z) * 2 + side for z in range(nz)]
-            )
+        keys(2, LAST_KEY)
+
+    @pl.when(core == 1)
+    def _():
+        with jax.named_scope("sum_z"):
+            all_of(zbuf.at[pl.ds(0, ring_z - 1)], sum_recv.at[2])
+        for h in range(n_head):
+            gbuf[h * heads : (h + 1) * heads] = total_of(zbuf, range(h * nz, h * nz + nz))
+        result_copy().start()
+
+    with jax.named_scope("key"):
+        keys(LAST_KEY, groups)
+
+    @pl.when(core == 0)
+    def _():
+        with jax.named_scope("sum_z"):
+            result_copy().wait_recv()
+
+    gb_ref[...] = gbuf[...]
 
     with jax.named_scope("drain"):
         for n in range(3):
@@ -475,10 +532,17 @@
                 id_copy(s).wait_send()
                 mask_copy(s).wait_send()
 
-        all_of(xbuf.at[pl.ds(0, row - 1)], sum_send.at[0])
-        if ny > 1:
-            all_of(ybuf.at[pl.ds(0, ny - 1)], sum_send.at[1])
-        all_of(zbuf.at[pl.ds(0, ring_z - 1)], sum_send.at[2])
+        @pl.when(core == 0)
+        def _():
+            pair_copy().wait_send()
+
+        @pl.when(core == 1)
+        def _():
+            all_of(xbuf.at[pl.ds(0, nx - 1)], sum_send.at[0])
+            if ny > 1:
+                all_of(ybuf.at[pl.ds(0, ny - 1)], sum_send.at[1])
+            all_of(zbuf.at[pl.ds(0, ring_z - 1)], sum_send.at[2])
+            result_copy().wait_send()
 
 
 def put_out(*refs):
@@ -499,8 +563,6 @@
         heads, buckets = bias_table.shape
         groups = width // 128
         sizes = (n_seq, nx, ny, nz, n_head, heads, groups)
-        row = 2 * nx
-        ring_z = n_head * nz * 2
         operands = (queries, keys, values, grad_out, bias_table, bucket_ids, block_mask)
         V = pltpu.VMEM
         dma = pltpu.SemaphoreType.DMA
@@ -508,14 +570,14 @@
             V((groups, 512, 256), BF16), V((groups, 512, 256), BF16),
             V((heads, 128), F32), V((4, 4, 256), jnp.int32), V((4, 1, 4), jnp.int32),
             V((7, heads, 256), F32), V((groups, 512, 256), F32), V((groups, 256, 384), F32),
-            V((512, 256), F32), V((512, 256), F32), V((512, 256), BF16), V((128, 256), BF16),
+            V((512, 256), F32), V((512, 256), F32), V((groups, 512, 256), BF16), V((groups, 128, 256), BF16),
             V((256, 384), F32), V((256, 384), F32), V((256, 384), BF16), V((256, 384), BF16),
             V((groups, 128, 128), F32), V((groups, 128, 128), F32),
             V((4, groups, 8, 128), F32), V((4, heads, 256), F32),
-            V((heads, 128), F32), V((row, heads // 2, 128), F32), V((ny, heads // 2, 128), F32),
-            V((ring_z, heads // 2, 128), F32),
+            V((heads, 128), F32), V((heads, 128), F32), V((nx, heads, 128), F32), V((ny, heads, 128), F32),
+            V((n_head * nz, heads, 128), F32), V((n_head * heads, 128), F32),
             dma((2, 2)), dma((3,)), dma((3,)), dma((3, groups)), dma((3,)), dma((groups,)), dma((2, 2)),
-            dma((3,)), dma((3, 2)), dma((2, 3)), dma((2, 3)), dma((3,)), dma((3,)),
+            dma((3,)), dma((3, 2)), dma((2, 3)), dma((2, 3)), dma((5,)), dma((5,)),
         ]
         in_hbm = pl.BlockSpec(memory_space=pltpu.HBM)
         in_vmem = pl.BlockSpec(memory_space=pltpu.VMEM)

time: 45.4 us -> 44.4 us (0.978)
  Pallas kernels: 44.6 us -> 43.5 us
    pallas_call x1, Pallas kernels: 43.6 us -> 42.6 us  [body(): pl.pallas_call(functools.partial(kernel, sizes), out_shape=shapes, in_spe...]
where the time goes in v5:
time: 44.4 us; the launch traced here: 44.2 us
  Pallas kernels  43.5 us (98%)
  between operations  0.64 us (1%)
    pallas_call x1, Pallas kernels, body(): pl.pallas_call(functools.partial(kernel, sizes), out_shape=shapes, in_spe...  42.6 us
    pallas_call x1, Pallas kernels, body(): pl.pallas_call(put_out, out_shape=shapes, in_specs=[in_vmem] * 4, out_spe...  0.91 us

profile of v5, /device:TPU:1, one launch (start us, length us, event | category | flops | bytes accessed | tf_op | source)
XLA Modules:
  0.0 44.2 jit_solution(7954411856864222966)
XLA Ops:
  0.6 42.6 %shard_map.102 = (bf16[128,1024]{1,0:T(8,128)(2,1)S(1)}, bf16[128,1024]{1,0:T(8,128)(2,1)S(1)}, bf16[128,1024]{1,0:T(8,128)(2,1)S(1)}, f32[32,128]{1,0:T(8,128)S(1)}) custom-call(bf16[128,1024]{1,0:T(8,128)(2,1)} %q_hbm.1, bf16[128,1024]{1,0:T(8,128)(2,1)} %k_hbm.1, bf16[128,1024]{1,0:T(8,128)(2,1)} %v_hbm.1, bf16[128,1024]{1,0:T(8,128)(2,1)} %do_hbm.1, ...), custom_call_target="tpu_custom_call" | custom-call | tf_op jit(solution)/shard_map/pallas_call | solution.py:586
  43.3 0.9 %shard_map.103 = (bf16[128,1024]{1,0:T(8,128)(2,1)}, bf16[128,1024]{1,0:T(8,128)(2,1)}, bf16[128,1024]{1,0:T(8,128)(2,1)}, f32[32,128]{1,0:T(8,128)}) custom-call(bf16[128,1024]{1,0:T(8,128)(2,1)S(1)} %get-tuple-element.8.refs_0_, bf16[128,1024]{1,0:T(8,128)(2,1)S(1)} %get-tuple-element.9.refs_1_, bf16[128,1024]{1,0:T(8,128)(2,1)S(1)} %get-tuple-element.10.refs_2_, ...), custom_call_target="tpu_custom_call" | custom-call | tf_op jit(solution)/shard_map/pallas_call | solution.py:596

commit v6 on v5

--- a/solution.py
+++ b/solution.py
@@ -16,7 +16,7 @@
 RELAY = 2
 FIRST = 3
 DEFER = 4
-LAST_KEY = 7
+LAST_KEY = 6
 NT = (((1,), (1,)), ((), ()))
 
 
@@ -76,11 +76,6 @@
     def signal(other):
         pl.semaphore_signal(barrier, inc=1, device_id=other, device_id_type=MESH)
 
-    @pl.when(core == 1)
-    def _():
-        for t in far_first(ring_z):
-            signal(z_partner(t))
-
     def all_of(ref, sem):
         pltpu.make_async_copy(ref, ref, sem).wait()
 
@@ -98,6 +93,12 @@
             all_of(buf.at[pl.ds(start, count), pl.ds(0, T)], load_sem.at[part, n])
 
     load(range(FIRST), 0)
+
+    @pl.when(core == 1)
+    def _():
+        for t in far_first(ring_z):
+            signal(z_partner(t))
+
     small = [
         pltpu.make_async_copy(table_hbm, tableb, small_sem.at[0]),
         pltpu.make_async_copy(ids_hbm.at[0], idsb.at[0], small_sem.at[1]),
@@ -117,7 +118,6 @@
     for o in (3, 2, 1):
         pl.when(me >= o)(lambda o=o: signal({"seq": me - o}))
         pl.when(me + o < n_seq)(lambda o=o: signal({"seq": me + o}))
-    load(range(FIRST, groups), 1)
 
     def remote(src, dst, send, recv, device):
         return pltpu.make_async_remote_copy(
@@ -192,16 +192,17 @@
             copy.wait()
     with jax.named_scope("barrier"):
         pl.semaphore_wait(barrier, near + core * (ring_z + ny + nx - 3))
-    for s in (1, 2, 3):
-
-        @pl.when(me >= s)
-        def _():
-            id_copy(s).start()
-            mask_copy(s).start()
-
     for g in range(FIRST):
         send_own(g)
-    loaded(FIRST, groups - FIRST, 1)
+        if g == 0:
+            for s in (1, 2, 3):
+
+                @pl.when(me >= s)
+                def _():
+                    id_copy(s).start()
+                    mask_copy(s).start()
+
+    load(range(FIRST, groups), 1)
     for s in (1, 2, 3):
 
         @pl.when(me < s)
@@ -267,6 +268,7 @@
 
     with jax.named_scope("build_query"):
         lax.fori_loop(0, groups, build_query, 0)
+    loaded(FIRST, groups - FIRST, 1)
     send_own(FIRST)
     with jax.named_scope("relay_first"):
         for g in range(RELAY):
@@ -456,6 +458,15 @@
     def _():
         pair_copy().start()
 
+    with jax.named_scope("grads"):
+        st_start(groups - 1)
+
+        def late(g, carry):
+            query_grads(g)
+            return carry
+
+        lax.fori_loop(groups - DEFER, groups, late, 0)
+
     @pl.when(core == 1)
     def _():
         with jax.named_scope("sum_pair"):
@@ -464,14 +475,8 @@
         for t in far_first(nx):
             x_copy(t).start()
 
-    with jax.named_scope("grads"):
-        st_start(groups - 1)
-
-        def late(g, carry):
-            query_grads(g)
-            return carry
-
-        lax.fori_loop(groups - DEFER, groups, late, 0)
+    with jax.named_scope("build_key"):
+        lax.fori_loop(0, groups - 2, build_key, 0)
 
     @pl.when(core == 1)
     def _():
@@ -482,7 +487,11 @@
             y_copy(t).start()
 
     with jax.named_scope("build_key"):
-        lax.fori_loop(0, groups, build_key, 0)
+        lax.fori_loop(groups - 2, groups, build_key, 0)
+    with jax.named_scope("key_wait"):
+        key_ready(0)
+    with jax.named_scope("key"):
+        keys(0, 2)
 
     @pl.when(core == 1)
     def _():
@@ -493,10 +502,6 @@
         for t in far_first(ring_z):
             z_copy(t).start()
 
-    with jax.named_scope("key_wait"):
-        key_ready(0)
-    with jax.named_scope("key"):
-        keys(0, 2)
     with jax.named_scope("key_wait"):
         key_ready(1)
     with jax.named_scope("key"):

time: 44.4 us -> 44.1 us (level)
  no operation moved by 1% of the time
where the time goes in v6:
time: 44.1 us; the launch traced here: 43.9 us
  Pallas kernels  43.3 us (98%)
  between operations  0.64 us (1%)
    pallas_call x1, Pallas kernels, body(): pl.pallas_call(functools.partial(kernel, sizes), out_shape=shapes, in_spe...  42.3 us
    pallas_call x1, Pallas kernels, body(): pl.pallas_call(put_out, out_shape=shapes, in_specs=[in_vmem] * 4, out_spe...  0.91 us

profile of v6, /device:TPU:1, one launch (start us, length us, event | category | flops | bytes accessed | tf_op | source)
XLA Modules:
  0.0 43.9 jit_solution(10827279572204739926)
XLA Ops:
  0.6 42.3 %shard_map.102 = (bf16[128,1024]{1,0:T(8,128)(2,1)S(1)}, bf16[128,1024]{1,0:T(8,128)(2,1)S(1)}, bf16[128,1024]{1,0:T(8,128)(2,1)S(1)}, f32[32,128]{1,0:T(8,128)S(1)}) custom-call(bf16[128,1024]{1,0:T(8,128)(2,1)} %q_hbm.1, bf16[128,1024]{1,0:T(8,128)(2,1)} %k_hbm.1, bf16[128,1024]{1,0:T(8,128)(2,1)} %v_hbm.1, bf16[128,1024]{1,0:T(8,128)(2,1)} %do_hbm.1, ...), custom_call_target="tpu_custom_call" | custom-call | tf_op jit(solution)/shard_map/pallas_call | solution.py:591
  43.0 0.9 %shard_map.103 = (bf16[128,1024]{1,0:T(8,128)(2,1)}, bf16[128,1024]{1,0:T(8,128)(2,1)}, bf16[128,1024]{1,0:T(8,128)(2,1)}, f32[32,128]{1,0:T(8,128)}) custom-call(bf16[128,1024]{1,0:T(8,128)(2,1)S(1)} %get-tuple-element.8.refs_0_, bf16[128,1024]{1,0:T(8,128)(2,1)S(1)} %get-tuple-element.9.refs_1_, bf16[128,1024]{1,0:T(8,128)(2,1)S(1)} %get-tuple-element.10.refs_2_, ...), custom_call_target="tpu_custom_call" | custom-call | tf_op jit(solution)/shard_map/pallas_call | solution.py:601

commit v7 on v6

--- a/solution.py
+++ b/solution.py
@@ -17,6 +17,7 @@
 FIRST = 3
 DEFER = 4
 LAST_KEY = 6
+PIECES = 4
 NT = (((1,), (1,)), ((), ()))
 
 
@@ -552,7 +553,12 @@
 
 def put_out(*refs):
     sems = refs[8]
-    copies = [pltpu.make_async_copy(refs[i], refs[4 + i], sems.at[i]) for i in range(4)]
+    pieces = [(i, r) for r in range(PIECES) for i in range(3)]
+    copies = [pltpu.make_async_copy(refs[3], refs[7], sems.at[3 * PIECES])]
+    for n, (i, r) in enumerate(pieces):
+        size = refs[i].shape[0] // PIECES
+        rows = pl.ds(r * size, size)
+        copies.append(pltpu.make_async_copy(refs[i].at[rows], refs[4 + i].at[rows], sems.at[n]))
     for copy in copies:
         copy.start()
     for copy in copies:
@@ -603,7 +609,7 @@
             out_shape=shapes,
             in_specs=[in_vmem] * 4,
             out_specs=(pl.BlockSpec(memory_space=pltpu.HBM),) * 4,
-            scratch_shapes=[dma((4,))],
+            scratch_shapes=[dma((3 * PIECES + 1,))],
         )(*(pltpu.with_memory_space_constraint(x, pltpu.VMEM) for x in results))
 
     block = P("seq", "head")

time: 44.1 us -> 44.1 us (level)
  no operation moved by 1% of the time
where the time goes in v7:
time: 44.1 us; the launch traced here: 44 us
  Pallas kernels  43.3 us (98%)
  between operations  0.64 us (1%)
    pallas_call x1, Pallas kernels, body(): pl.pallas_call(functools.partial(kernel, sizes), out_shape=shapes, in_spe...  42.3 us
    pallas_call x1, Pallas kernels, body(): pl.pallas_call(put_out, out_shape=shapes, in_specs=[in_vmem] * 4, out_spe...  0.98 us

profile of v7, /device:TPU:1, one launch (start us, length us, event | category | flops | bytes accessed | tf_op | source)
XLA Modules:
  0.0 44.0 jit_solution(9992494765917507013)
XLA Ops:
  0.6 42.3 %shard_map.102 = (bf16[128,1024]{1,0:T(8,128)(2,1)S(1)}, bf16[128,1024]{1,0:T(8,128)(2,1)S(1)}, bf16[128,1024]{1,0:T(8,128)(2,1)S(1)}, f32[32,128]{1,0:T(8,128)S(1)}) custom-call(bf16[128,1024]{1,0:T(8,128)(2,1)} %q_hbm.1, bf16[128,1024]{1,0:T(8,128)(2,1)} %k_hbm.1, bf16[128,1024]{1,0:T(8,128)(2,1)} %v_hbm.1, bf16[128,1024]{1,0:T(8,128)(2,1)} %do_hbm.1, ...), custom_call_target="tpu_custom_call" | custom-call | tf_op jit(solution)/shard_map/pallas_call | solution.py:597
  43.0 1.0 %shard_map.103 = (bf16[128,1024]{1,0:T(8,128)(2,1)}, bf16[128,1024]{1,0:T(8,128)(2,1)}, bf16[128,1024]{1,0:T(8,128)(2,1)}, f32[32,128]{1,0:T(8,128)}) custom-call(bf16[128,1024]{1,0:T(8,128)(2,1)S(1)} %get-tuple-element.8.refs_0_, bf16[128,1024]{1,0:T(8,128)(2,1)S(1)} %get-tuple-element.9.refs_1_, bf16[128,1024]{1,0:T(8,128)(2,1)S(1)} %get-tuple-element.10.refs_2_, ...), custom_call_target="tpu_custom_call" | custom-call | tf_op jit(solution)/shard_map/pallas_call | solution.py:607
